TPU v7x, 512 devices: a whole 4x8x8 slice. The times are simulated.
512 devices in a mesh: blk: 128 (over z_lo, y, x), freq: 4 (over z_hi, core).
Axes of the slice: x: 4, y: 8, z: 8 (z_hi: 2, z_lo: 4; z = z_hi * 4 + z_lo), core: 2. Of those that a mesh axis runs over, the one named last changes fastest.
Arguments:
- node_index: int32 [3, 16384], P(None, 'blk'), may hold values from 0 to 63
- emitters: int32 [64], replicated, may hold values from 0 to 16383
- admittance: float32 [2, 16384], P(None, 'blk'), may hold values from -3 to 3
- wavenumbers: float32 [4], P('freq'), may hold values from 20 to 60
Outputs:
- scattered: bfloat16 [4, 2, 64, 16384], P('freq', None, None, 'blk')
- gradient: float32 [16384], P('blk')
All inputs are finite; a program needn't handle non-finite values.
Results may differ from a plain program's by a relative error of at most 0.006.
Values may be sent and summed in bfloat16 or wider, within the bound.
No kernel may reach another device: no remote copies, remote signals or barrier semaphores. Data moves between devices by JAX's collectives and lax.ppermute only.
A program may use at most 64 MiB of HBM per device.

v0:
```python
import jax
import jax.numpy as jnp
from jax import lax
from jax.sharding import Mesh
from jax.sharding import PartitionSpec as P

GRID = 64
BLK = ("blk_0", "blk_1", "blk_2")


soften = 0.0025


def in_order(blocks, dim):
    blocks = jnp.moveaxis(blocks, 0, dim)
    shape = blocks.shape
    return blocks.reshape(*shape[:dim], shape[dim] * shape[dim + 1], *shape[dim + 2 :])


def all_blocks(value, axes, turns):
    blocks = value
    for k in turns:
        blocks = lax.all_gather(blocks, axes[k])
    done = turns[::-1]
    back = [done.index(k) for k in range(len(axes))]
    blocks = blocks.transpose(*back, *range(len(axes), blocks.ndim))
    return blocks.reshape(-1, *value.shape)


def gather_axes(value, axes, turns, dim):
    return in_order(all_blocks(value, axes, turns), dim)


def copy_for_each(value, axis):
    copies = jnp.broadcast_to(value, (lax.axis_size(axis), *value.shape))
    return lax.all_to_all(copies, axis, split_axis=0, concat_axis=0, tiled=True)


def taken_together(value, axis):
    return copy_for_each(value, axis).sum(axis=0)


def green_tile(row_places, col_places, wavenum, strength):
    separation = row_places[:, :, None] - col_places[:, None, :]
    radius = jnp.sqrt(jnp.sum(separation * separation, axis=0) + soften)
    amplitude = strength / radius
    phase_turn = wavenum * radius
    return jnp.stack([amplitude * jnp.cos(phase_turn), amplitude * jnp.sin(phase_turn)]).astype(
        jnp.bfloat16
    )


def apply_tile(tile_data, source):
    real_part = jnp.einsum(
        "tc,rc->tr", source[0], tile_data[0], preferred_element_type=jnp.float32
    ) - jnp.einsum("tc,rc->tr", source[1], tile_data[1], preferred_element_type=jnp.float32)
    imag_part = jnp.einsum(
        "tc,rc->tr", source[1], tile_data[0], preferred_element_type=jnp.float32
    ) + jnp.einsum("tc,rc->tr", source[0], tile_data[1], preferred_element_type=jnp.float32)
    return jnp.stack([real_part, imag_part])


def complex_scale(factor_pair, field_pair):
    factor_real = factor_pair[0][None, :]
    factor_imag = factor_pair[1][None, :]
    real_part = factor_real * field_pair[0] - factor_imag * field_pair[1]
    imag_part = factor_real * field_pair[1] + factor_imag * field_pair[0]
    return jnp.stack([real_part, imag_part])


def row_potential(places, own_places, wavenum, strength, block_count, row_count):
    group_blocks = 1
    for candidate in range(1, block_count + 1):
        if block_count % candidate == 0 and candidate * row_count <= 4096:
            group_blocks = candidate
    group_cols = group_blocks * row_count

    def make_tile(group_id):
        col_places = lax.dynamic_slice_in_dim(places, group_id * group_cols, group_cols, 1)
        return green_tile(own_places, col_places, wavenum, strength)

    tile_stack = lax.map(make_tile, jnp.arange(block_count // group_blocks, dtype=jnp.int32))
    tile_flat = jnp.transpose(tile_stack, (1, 2, 0, 3)).reshape(
        2, row_count, block_count * row_count
    )

    def potential(source, whole_source):
        if whole_source is None:
            whole_source = gather_axes(source, BLK, (0, 1, 2), 2)
        return apply_tile(tile_flat, whole_source)

    return potential


def local(node_index, emitters, admittance, wavenumbers):
    block_count = lax.axis_size(BLK)
    lane_count = lax.axis_size("freq")
    row_count = node_index.shape[1]
    node_count = block_count * row_count
    emitter_count = emitters.shape[0]
    own_block = lax.axis_index(BLK)
    every_index = lax.all_gather(node_index, BLK, axis=1, tiled=True)
    places = every_index.astype(jnp.float32) / GRID
    own_places = node_index.astype(jnp.float32) / GRID
    wavenum = wavenumbers[0]
    strength = float(node_count) ** (-0.5)
    emitter_places = places[:, emitters]
    incident_whole = green_tile(emitter_places, places, wavenum, 1.0)
    incident = lax.dynamic_slice_in_dim(incident_whole, own_block * row_count, row_count, 2)
    potential = row_potential(places, own_places, wavenum, strength, block_count, row_count)
    first_wave = potential(incident, incident_whole)
    weighted = complex_scale(admittance, first_wave).astype(jnp.bfloat16)
    second = potential(weighted, None)
    lane_terms = jnp.sum(first_wave[0] * second[0] - first_wave[1] * second[1], axis=0) / (
        lane_count * emitter_count
    )
    gradient = taken_together(lane_terms, "freq")
    return (second.astype(jnp.bfloat16)[None], gradient)


def solution(mesh):
    split = Mesh(
        mesh.devices.reshape(4, 8, 4, mesh.shape["freq"]), ("blk_0", "blk_1", "blk_2", "freq")
    )
    in_specs = (P(None, BLK), P(), P(None, BLK), P("freq"))
    out_specs = (P("freq", None, None, BLK), P(BLK))
    return jax.shard_map(local, mesh=split, in_specs=in_specs, out_specs=out_specs, check_vma=False)
```

profile of v0, /device:TPU:1, one launch (start us, length us, event | category | flops | bytes accessed | tf_op | source)
XLA Modules:
  0.0 678.0 jit_solution(9046614232390934011)
XLA Ops:
  7.2 0.8 copy.41
  8.7 366.5 %all_gather.19 = s32[3,16384]{0,1:T(8,128)S(1)} all-gather(s32[3,128]{0,1:T(8,128)S(1)} %copy.41), channel_id=1, replica_groups=mesh['blk_0'=4,'blk_1'=8,'blk_2'=4,'freq'=4] {'blk_0','blk_1','blk_2'}, dimensions={1}, use_global_device_ids=true | all-gather | bytes 198144 | tf_op jit(solution)/shard_map/all_gather | solution.py:102
  375.2 3.5 convert_multiply_fusion
  378.8 5.5 copy.43
  384.3 4.0 gather_fusion
  389.0 3.6 multiply_reduce_fusion.1
  392.5 68.6 %while.10 = (s32[]{:T(128)}, bf16[4,2,128,4096]{2,3,0,1:T(8,128)(2,1)}, f32[3,128]{1,0:T(4,128)S(1)}, s32[4]{0:T(128)S(1)}, f32[3,16384]{1,0:T(4,128)S(1)}, /*in...) while((s32[]{:T(128)}, bf16[4,2,128,4096]{2,3,0,1:T(8,128)(2,1)}, f32[3,128]{1,0:T(4,128)S(1)}, ...), condition=%wide.region_3.4_spmd, body=%wide.region_1.3_spmd.sunk | while | flops 8912902 | bytes 19023540 | solution.py:82
  393.8 0.9 multiply_reduce_fusion.3
  394.6 8.9 %fusion.43 = (bf16[1,1,128,4096]{3,2,1,0:T(8,128)(2,1)S(1)}, bf16[1,1,128,4096]{3,2,1,0:T(8,128)(2,1)S(1)}) fusion(f32[]{:T(128)} %get-tuple-element.164, f32[128,4096]{1,0:T(8,128)S(1)} %multiply_reduce_fusion.3), kind=kLoop, calls=%fused_computation.7.clone.1 | loop fusion | flops 3670016 | bytes 4194308 | tf_op jit(solution)/shard_map/while/body/eval_jaxpr/stack | solution.py:48
  403.6 1.5 pad_maximum_fusion.4
  405.1 3.1 copy.77
  408.2 1.4 constant_dynamic-update-slice_fusion.2
  410.9 0.9 multiply_reduce_fusion.3
  411.8 8.9 %fusion.43 = (bf16[1,1,128,4096]{3,2,1,0:T(8,128)(2,1)S(1)}, bf16[1,1,128,4096]{3,2,1,0:T(8,128)(2,1)S(1)}) fusion(f32[]{:T(128)} %get-tuple-element.164, f32[128,4096]{1,0:T(8,128)S(1)} %multiply_reduce_fusion.3), kind=kLoop, calls=%fused_computation.7.clone.1 | loop fusion | flops 3670016 | bytes 4194308 | tf_op jit(solution)/shard_map/while/body/eval_jaxpr/stack | solution.py:48
  420.7 1.5 pad_maximum_fusion.4
  422.2 3.1 copy.77
  425.4 1.5 constant_dynamic-update-slice_fusion.2
  428.1 0.9 multiply_reduce_fusion.3
  428.9 8.9 %fusion.43 = (bf16[1,1,128,4096]{3,2,1,0:T(8,128)(2,1)S(1)}, bf16[1,1,128,4096]{3,2,1,0:T(8,128)(2,1)S(1)}) fusion(f32[]{:T(128)} %get-tuple-element.164, f32[128,4096]{1,0:T(8,128)S(1)} %multiply_reduce_fusion.3), kind=kLoop, calls=%fused_computation.7.clone.1 | loop fusion | flops 3670016 | bytes 4194308 | tf_op jit(solution)/shard_map/while/body/eval_jaxpr/stack | solution.py:48
  437.9 1.5 pad_maximum_fusion.4
  439.4 3.1 copy.77
  442.5 1.5 constant_dynamic-update-slice_fusion.2
  445.2 0.9 multiply_reduce_fusion.3
  446.1 8.9 %fusion.43 = (bf16[1,1,128,4096]{3,2,1,0:T(8,128)(2,1)S(1)}, bf16[1,1,128,4096]{3,2,1,0:T(8,128)(2,1)S(1)}) fusion(f32[]{:T(128)} %get-tuple-element.164, f32[128,4096]{1,0:T(8,128)S(1)} %multiply_reduce_fusion.3), kind=kLoop, calls=%fused_computation.7.clone.1 | loop fusion | flops 3670016 | bytes 4194308 | tf_op jit(solution)/shard_map/while/body/eval_jaxpr/stack | solution.py:48
  455.0 1.5 pad_maximum_fusion.4
  456.6 3.1 copy.77
  459.7 1.5 constant_dynamic-update-slice_fusion.2
  461.2 3.9 fusion.24
  465.1 0.7 copy-done.4
  465.8 16.6 %multiply_convert_fusion.2 = (bf16[64,16384]{1,0:T(8,128)(2,1)S(1)}, bf16[64,16384]{1,0:T(8,128)(2,1)S(1)}) fusion(f32[64,16384]{1,0:T(8,128)S(1)} %copy-done.4, f32[]{:T(128)} %bitcast.66), kind=kLoop, calls=%fused_computation.13 | loop fusion | flops 7340032 | bytes 8388612 | tf_op jit(solution)/shard_map/slice | solution.py:56
  482.5 0.9 fusion.29
  483.3 0.9 fusion.28
  484.2 0.9 convolution_add_fusion
  485.1 0.9 convolution_subtract_fusion
  486.0 11.2 %all_gather.20 = bf16[4,2,64,128]{3,2,1,0:T(8,128)(2,1)} all-gather(bf16[1,2,64,128]{3,2,1,0:T(8,128)(2,1)S(1)} %pad_maximum_fusion.1), channel_id=1, replica_groups=mesh['blk_0'=4,'blk_1'=8,'blk_2'=4,'freq'=4] {'blk_0'}, dimensions={0}, use_global_device_ids=true | all-gather | bytes 163840 | tf_op jit(solution)/shard_map/all_gather | solution.py:23
  497.4 84.1 %all-gather.5.cloned.1.call-done = bf16[32,2,64,128]{3,2,1,0:T(8,128)(2,1)} async-done(((bf16[4,2,64,128]{3,2,1,0:T(8,128)(2,1)}), bf16[32,2,64,128]{3,2,1,0:T(8,128)(2,1)}) %all-gather.5.cloned.1.call-update) | async-done | bytes 1048592 | tf_op jit(solution)/shard_map/all_gather | solution.py:23
  581.6 59.3 %all-gather.7.cloned.1.call-done = bf16[32,4,2,64,128]{4,3,2,1,0:T(8,128)(2,1)} async-done(((bf16[8,4,2,64,128]{4,3,2,1,0:T(8,128)(2,1)}), bf16[32,4,2,64,128]{4,3,2,1,0:T(8,128)(2,1)}) %all-gather.7.cloned.1.call-update) | async-done | bytes 4194320 | tf_op jit(solution)/shard_map/all_gather | solution.py:23
  640.8 3.1 copy.46
  644.0 1.0 fusion.25
  645.0 1.4 copy.48
  646.3 0.8 copy-done.1
  647.2 1.6 fusion.6
  648.8 1.6 fusion.4
  650.4 1.4 copy.47
  651.7 1.6 fusion.16
  653.3 1.5 subtract_reduce_fusion
  655.5 8.2 %all-to-all-start = ((f32[4,1,128]{2,1,0:T(1,128)}), f32[4,1,128]{2,1,0:T(1,128)S(1)}, u32[]{:S(2)}, u32[]{:S(2)}) async-start(f32[4,1,128]{2,1,0:T(1,128)} %broadcast_in_dim.18), calls=%async_computation | async-start | bytes 4096 | tf_op jit(solution)/shard_map/all_to_all | solution.py:36
  664.3 6.4 all-to-all-done
  (37 shorter events, 5.3 us)
Async XLA Ops:
  7.2 574.4 %all-gather.5.cloned.1.call-start = ((), (), s32[]{:S(2)}) async-start(), calls=%async_computation.1 | async-start | bytes 1179648 | tf_op jit(solution)/shard_map/all_gather | solution.py:23
  378.8 5.5 copy-start.6
  461.2 4.7 copy-start.4
  465.1 18.2 %copy-start.2 = (bf16[1,128,4,4096]{1,3,2,0:T(8,128)(2,1)}, bf16[1,128,4,4096]{1,3,2,0:T(8,128)(2,1)S(1)}, u32[]{:S(2)}) copy-start(bf16[1,128,4,4096]{1,3,2,0:T(8,128)(2,1)S(1)} %get-tuple-element.86) | copy-start | bytes 12582916
  465.1 20.0 %copy-start = (bf16[1,128,4,4096]{1,3,2,0:T(8,128)(2,1)}, bf16[1,128,4,4096]{1,3,2,0:T(8,128)(2,1)S(1)}, u32[]{:S(2)}) copy-start(bf16[1,128,4,4096]{1,3,2,0:T(8,128)(2,1)S(1)} %get-tuple-element.85) | copy-start | bytes 12582916
  485.1 0.9 copy-start.5
  497.2 143.6 %all-gather.7.cloned.1.call-start = ((), (), s32[]{:S(2)}) async-start(), calls=%async_computation.2 | async-start | bytes 5242880 | tf_op jit(solution)/shard_map/all_gather | solution.py:23
  645.0 2.2 copy-start.1
  646.3 2.4 copy-start.3
  655.5 15.2 %all-to-all-start = ((f32[4,1,128]{2,1,0:T(1,128)}), f32[4,1,128]{2,1,0:T(1,128)S(1)}, u32[]{:S(2)}, u32[]{:S(2)}) async-start(f32[4,1,128]{2,1,0:T(1,128)} %broadcast_in_dim.18), calls=%async_computation | async-start | bytes 4096 | tf_op jit(solution)/shard_map/all_to_all | solution.py:36
Sparse Core Ops, SparseCore 0:
  497.3 84.1 all-gather.4
  583.6 57.1 all-gather.6
where the time goes:
time: 679 us; the launch traced here: 678 us
  blocking collectives  378 us (56%)
  waiting for transfers between devices  150 us (22%)
  other arithmetic  70.8 us (10%)
  local copies, waits for them, and re-layouts  43.9 us (6%)
  between operations  14.9 us (2%)
  matrix products  9.74 us (1%)
  starting transfers between devices  8.47 us (1%)
    all_gather x1, blocking collectives, local(): every_index = lax.all_gather(node_index, BLK, axis=1, tiled=True)  367 us
    all_gather x2, waiting for transfers between devices, all_blocks(): blocks = lax.all_gather(blocks, axes[k])  143 us
    another operation x8, other arithmetic, green_tile(): jnp.stack([amplitude * jnp.cos(phase_turn), amplitude * jnp.sin(phase_tur...  41.8 us
    dynamic_update_slice x8, local copies, waits for them, and re-layouts, row_potential(): lax.map(make_tile, jnp.arange(block_count // group_blocks, dtype=jnp.int32))  18.3 us
    slice x1, other arithmetic, apply_tile(): source[1]  16.6 us
  transfers between devices with their start and end apart: 3, of which 3 were waited for; matrix products, arithmetic and copies ran while one was open for 0% of the time, Pallas kernels for 0%

commit v1 on v0

v1 whole, which is shorter than its diff:
```python
import math

import jax
import jax.numpy as jnp
from jax import lax
from jax.experimental import pallas as pl
from jax.experimental.pallas import tpu as pltpu
from jax.sharding import Mesh
from jax.sharding import PartitionSpec as P

GRID = 64
BLK = ("z", "y", "x")
GATHER = ("z", "x")
REDUCE = "y"
LANES = 128
FEATURES = 16
SOFT = 0.0025 * GRID * GRID
MAGIC = 12582912.0
ROOT2 = math.sqrt(2.0)
SIN_POLY = [ROOT2 * c for c in (3.1415820221197075, -5.167142794757069, 2.541899010399708, -0.554636148527055)]
COS_POLY = [ROOT2 * c for c in (0.9999933001981278, -4.933938170377516, 4.04128504935244, -1.2221298133692595)]


def poly(coefs, s):
    total = coefs[-1] * s + coefs[-2]
    for c in coefs[-3::-1]:
        total = total * s + c
    return total


def green_parts(square, turns_per_step):
    v = square + SOFT
    inv = lax.rsqrt(v)
    turns = (v * inv) * turns_per_step
    f = turns - ((turns + MAGIC) - MAGIC)
    s = f * f
    half_sin = poly(SIN_POLY, s) * f
    half_cos = poly(COS_POLY, s)
    q = inv * half_sin
    return inv - q * half_sin, q * half_cos


def centred(places):
    return places.astype(jnp.float32) - 32.0


def column_features(places):
    p = centred(places)
    n = jnp.sum(p * p, axis=0, keepdims=True)
    high = ((n * (1 / 64) + MAGIC) - MAGIC) * 64.0
    low = n - high
    one = jnp.ones_like(n)
    zero = jnp.zeros((FEATURES - 7, n.shape[1]), jnp.float32)
    return jnp.concatenate([p * -2.0, one, one, high, low, zero], axis=0)


def row_features(x, y, z):
    lane = lax.broadcasted_iota(jnp.int32, x.shape, 1)
    x, y, z = x - 32.0, y - 32.0, z - 32.0
    n = x * x + y * y + z * z
    high = ((n * (1 / 64) + MAGIC) - MAGIC) * 64.0
    low = n - high
    out = jnp.where(lane == 0, x, 0.0)
    out = jnp.where(lane == 1, y, out)
    out = jnp.where(lane == 2, z, out)
    out = jnp.where(lane == 3, high, out)
    out = jnp.where(lane == 4, low, out)
    return jnp.where((lane == 5) | (lane == 6), 1.0, out)


def dot(a, b, contract=((1,), (0,))):
    return lax.dot_general(a, b, (contract, ((), ())), preferred_element_type=jnp.float32)


NT = ((1,), (1,))


def rows_of(places):
    count = places.shape[1]
    spread = []
    for d in range(3):
        line = jnp.broadcast_to(places[d : d + 1, :].astype(jnp.float32), (LANES, count))
        spread.append(jnp.transpose(line))
    return spread


def first_kernel(turns_ref, places_ref, own_ref, emitters_ref, admittance_ref, first_ref, weighted_ref,
                 cols_ref, rows_ref, d0, d1, g0, g1, acc_ref):
    blocks = places_ref.shape[0]
    own = own_ref.shape[1]
    emitters = emitters_ref.shape[0]
    width = d0.shape[1]
    per = width // own
    chunks = blocks // per
    turns = turns_ref[0] * (1.0 / (GRID * 2.0 * math.pi))

    rows_ref[0:own] = row_features(*rows_of(own_ref[...])).astype(jnp.bfloat16)
    index = jnp.broadcast_to(emitters_ref[...], (emitters, LANES))
    lane = lax.broadcasted_iota(jnp.int32, (emitters, LANES), 1)
    of_block = jnp.where(lane == index // own, 1.0, 0.0).astype(jnp.bfloat16)
    at_lane = lane == index % own
    every = jnp.ones((LANES, LANES), jnp.bfloat16)
    found = []
    for d in range(3):
        line = dot(of_block, places_ref[:, d, :])
        found.append(dot(jnp.where(at_lane, line, 0.0).astype(jnp.bfloat16), every))
    rows_ref[own : own + emitters] = row_features(*found).astype(jnp.bfloat16)

    acc_ref[...] = jnp.zeros_like(acc_ref)

    def distances(chunk, d_ref):
        for b in range(per):
            cols = column_features(places_ref[chunk * per + b]).astype(jnp.bfloat16)
            d_ref[:, b * own : (b + 1) * own] = dot(rows_ref[:, 0:FEATURES], cols)

    def tile(d_ref, g_ref):
        for r in range(0, own + emitters, 16):
            real, imag = green_parts(d_ref[r : r + 16, :], turns)
            at = r if r < own else r + own
            step = own if r < own else emitters
            g_ref[at : at + 16, :] = real.astype(jnp.bfloat16)
            g_ref[at + step : at + step + 16, :] = imag.astype(jnp.bfloat16)

    def gather(g_ref):
        acc_ref[...] += dot(g_ref[2 * own :, :], g_ref[0 : 2 * own, :], NT)

    distances(0, d0)
    g1[...] = jnp.zeros_like(g1)

    def pair(i, carry):
        distances(2 * i + 1, d1)
        tile(d0, g0)
        gather(g1)
        distances(jnp.minimum(2 * i + 2, chunks - 1), d0)
        tile(d1, g1)
        gather(g0)
        return carry

    lax.fori_loop(0, chunks // 2, pair, 0)
    gather(g1)
    scale = (GRID * GRID) * float(blocks * own) ** (-0.5)
    top, low = acc_ref[0:emitters, :], acc_ref[emitters:, :]
    real = (top[:, 0:own] - low[:, own:]) * scale
    imag = (low[:, 0:own] + top[:, own:]) * scale
    first_ref[0] = real
    first_ref[1] = imag
    a, b = admittance_ref[0:1, :], admittance_ref[1:2, :]
    w_real = (a * real - b * imag).astype(jnp.bfloat16)
    w_imag = (a * imag + b * real).astype(jnp.bfloat16)
    for k in range(weighted_ref.shape[0]):
        weighted_ref[k, 0] = w_real
        weighted_ref[k, 1] = w_imag


def second_kernel(turns_ref, row_places_ref, col_places_ref, source_ref, part_ref,
                  cols_ref, rows_ref, d0, d1, r0, i0, r1, i1, acc_r, acc_i, *, node_count):
    groups, _, own = col_places_ref.shape
    targets = row_places_ref.shape[0]
    emitters = source_ref.shape[2]
    width = targets * own
    turns = turns_ref[0] * (1.0 / (GRID * 2.0 * math.pi))
    for b in range(targets):
        cols_ref[:, b * own : (b + 1) * own] = column_features(row_places_ref[b]).astype(jnp.bfloat16)
    acc_r[...] = jnp.zeros_like(acc_r)
    acc_i[...] = jnp.zeros_like(acc_i)

    def distances(c, d_ref):
        rows = row_features(*rows_of(col_places_ref[c])).astype(jnp.bfloat16)
        d_ref[...] = dot(rows[:, 0:FEATURES], cols_ref[...])

    def tile(d_ref, r_ref, i_ref):
        for r in range(0, own, 16):
            for w in range(0, width, 512):
                real, imag = green_parts(d_ref[r : r + 16, w : w + 512], turns)
                r_ref[r : r + 16, w : w + 512] = real.astype(jnp.bfloat16)
                i_ref[r : r + 16, w : w + 512] = imag.astype(jnp.bfloat16)

    def gather(c, r_ref, i_ref):
        lhs = source_ref[c].reshape(2 * emitters, own)
        acc_r[...] += dot(lhs, r_ref[...])
        acc_i[...] += dot(lhs, i_ref[...])

    distances(0, d0)
    r1[...] = jnp.zeros_like(r1)
    i1[...] = jnp.zeros_like(i1)

    def pair(k, carry):
        distances(2 * k + 1, d1)
        tile(d0, r0, i0)
        gather(jnp.maximum(2 * k - 1, 0), r1, i1)
        distances(jnp.minimum(2 * k + 2, groups - 1), d0)
        tile(d1, r1, i1)
        gather(2 * k, r0, i0)
        return carry

    lax.fori_loop(0, groups // 2, pair, 0)
    gather(groups - 1, r1, i1)
    scale = GRID * float(node_count) ** (-0.5)
    for b in range(targets):
        at = slice(b * own, (b + 1) * own)
        part_ref[b, 0] = ((acc_r[0:emitters, at] - acc_i[emitters:, at]) * scale).astype(part_ref.dtype)
        part_ref[b, 1] = ((acc_r[emitters:, at] + acc_i[0:emitters, at]) * scale).astype(part_ref.dtype)


def last_kernel(parts_ref, first_ref, second_ref, terms_ref, *, share):
    real = parts_ref[0, 0].astype(jnp.float32)
    imag = parts_ref[0, 1].astype(jnp.float32)
    for b in range(1, parts_ref.shape[0]):
        real += parts_ref[b, 0].astype(jnp.float32)
        imag += parts_ref[b, 1].astype(jnp.float32)
    second_ref[0, 0] = real.astype(jnp.bfloat16)
    second_ref[0, 1] = imag.astype(jnp.bfloat16)
    terms = jnp.sum(first_ref[0] * real - first_ref[1] * imag, axis=0, keepdims=True) * share
    terms_ref[...] = jnp.broadcast_to(terms[None], terms_ref.shape)


VMEM = pl.BlockSpec(memory_space=pltpu.VMEM)
SMEM = pl.BlockSpec(memory_space=pltpu.SMEM)


def local(node_index, emitters, admittance, wavenumbers):
    sizes = [lax.axis_size(a) for a in BLK]
    blocks = sizes[0] * sizes[1] * sizes[2]
    lanes = lax.axis_size("freq")
    own = node_index.shape[1]
    count = blocks * own
    tx = emitters.shape[0]
    near, far = lax.axis_size(GATHER), lax.axis_size(REDUCE)

    own_places = node_index.astype(jnp.bfloat16)
    copies = jnp.broadcast_to(own_places, (blocks, *own_places.shape))
    places = lax.all_to_all(copies, BLK, split_axis=0, concat_axis=0, tiled=True)
    f32, bf16 = jnp.float32, jnp.bfloat16
    width = 4 * own
    first, weighted = pl.pallas_call(
        first_kernel,
        out_shape=(
            jax.ShapeDtypeStruct((2, tx, own), f32),
            jax.ShapeDtypeStruct((near, 2, tx, own), bf16),
        ),
        in_specs=[SMEM, VMEM, VMEM, VMEM, VMEM],
        out_specs=(VMEM, VMEM),
        scratch_shapes=[
            pltpu.VMEM((FEATURES, width), bf16),
            pltpu.VMEM((own + tx, LANES), bf16),
            pltpu.VMEM((own + tx, width), f32),
            pltpu.VMEM((own + tx, width), f32),
            pltpu.VMEM((2 * (own + tx), width), bf16),
            pltpu.VMEM((2 * (own + tx), width), bf16),
            pltpu.VMEM((2 * tx, 2 * own), f32),
        ],
        name="first_wave",
    )(wavenumbers, places, own_places, emitters[:, None], admittance)

    grouped = places.reshape(*sizes, 3, own)
    row_places = lax.dynamic_index_in_dim(
        lax.dynamic_index_in_dim(grouped, lax.axis_index("z"), 0, False), lax.axis_index("x"), 1, False
    )
    col_places = lax.dynamic_index_in_dim(grouped, lax.axis_index("y"), 1, False).reshape(near, 3, own)
    source = lax.all_to_all(weighted, GATHER, split_axis=0, concat_axis=0, tiled=True)
    import functools

    part = pl.pallas_call(
        functools.partial(second_kernel, node_count=count),
        out_shape=jax.ShapeDtypeStruct((far, 2, tx, own), bf16),
        in_specs=[SMEM, VMEM, VMEM, VMEM],
        out_specs=VMEM,
        scratch_shapes=[
            pltpu.VMEM((FEATURES, far * own), bf16),
            pltpu.VMEM((own, LANES), bf16),
            pltpu.VMEM((own, far * own), f32),
            pltpu.VMEM((own, far * own), f32),
            pltpu.VMEM((own, far * own), bf16),
            pltpu.VMEM((own, far * own), bf16),
            pltpu.VMEM((own, far * own), bf16),
            pltpu.VMEM((own, far * own), bf16),
            pltpu.VMEM((2 * tx, far * own), f32),
            pltpu.VMEM((2 * tx, far * own), f32),
        ],
        name="second_wave",
    )(wavenumbers, row_places, col_places, source)
    parts = lax.all_to_all(part, REDUCE, split_axis=0, concat_axis=0, tiled=True)
    second, terms = pl.pallas_call(
        functools.partial(last_kernel, share=1.0 / (lanes * tx)),
        out_shape=(
            jax.ShapeDtypeStruct((1, 2, tx, own), bf16),
            jax.ShapeDtypeStruct((lanes, 1, own), f32),
        ),
        in_specs=[VMEM, VMEM],
        out_specs=(VMEM, VMEM),
        name="last_sum",
    )(parts, first)
    terms = lax.all_to_all(terms, "freq", split_axis=0, concat_axis=0, tiled=True)
    return second, terms.sum(axis=(0, 1))


def solution(mesh):
    split = Mesh(mesh.devices.reshape(4, 8, 4, mesh.shape["freq"]), ("z", "y", "x", "freq"))
    in_specs = (P(None, BLK), P(), P(None, BLK), P("freq"))
    out_specs = (P("freq", None, None, BLK), P(BLK))
    return jax.shard_map(local, mesh=split, in_specs=in_specs, out_specs=out_specs, check_vma=False)
```

time: 679 us -> 116 us (0.17)
  blocking collectives: 378 us -> 32.7 us
  waiting for transfers between devices: 150 us -> 19.8 us
  other arithmetic: 70.8 us -> 1.22 us
  local copies, waits for them, and re-layouts: 43.9 us -> 6.1 us
  Pallas kernels: 0 us -> 32.8 us
  between operations: 14.9 us -> 1.32 us
  starting transfers between devices: 8.47 us -> 21.3 us
  matrix products: 9.74 us -> 0 us
    all_gather x2 -> x0, blocking collectives: 378 us -> none  [the longest x1 367 us: local(): every_index = lax.all_gather(node_index, BLK, axis=1, tiled=True)]
    all_gather x2 -> x0, waiting for transfers between devices: 143 us -> none  [all_blocks(): blocks = lax.all_gather(blocks, axes[k])]
    another operation x11 -> x0, other arithmetic: 42.4 us -> none  [the longest x8 41.8 us: green_tile(): jnp.stack([amplitude * jnp.cos(phase_turn), amplitude * jnp.sin(phase_tur...]
    pallas_call x0 -> x3, Pallas kernels: none -> 32.8 us  [the longest x1 16.8 us: local(): pl.pallas_call(first_kernel, out_shape=(jax.ShapeDtypeStruct((2, tx, own)...]
    all_to_all x0 -> x2, blocking collectives: none -> 32.7 us  [the longest x1 19.2 us: local(): lax.all_to_all(terms, 'freq', split_axis=0, concat_axis=0, tiled=True)]
    dynamic_update_slice x8 -> x0, local copies, waits for them, and re-layouts: 18.3 us -> none  [row_potential(): lax.map(make_tile, jnp.arange(block_count // group_blocks, dtype=jnp.int32))]
    slice x1 -> x0, other arithmetic: 16.6 us -> none  [apply_tile(): source[1]]
    all_to_all x1 -> x2, waiting for transfers between devices: 6.38 us -> 19.8 us  [the longest x1 10.2 us: local(): lax.all_to_all(weighted, GATHER, split_axis=0, concat_axis=0, tiled=True)]
  transfers between devices with their start and end apart: 3 -> 2, of which waited for: 3 -> 2; matrix products, arithmetic and copies ran while one was open for 0% -> 3% of each run, Pallas kernels for 0% -> 0%
where the time goes in v1:
time: 116 us; the launch traced here: 115 us
  Pallas kernels  32.8 us (28%)
  blocking collectives  32.7 us (28%)
  starting transfers between devices  21.3 us (18%)
  waiting for transfers between devices  19.8 us (17%)
  local copies, waits for them, and re-layouts  6.1 us (5%)
  between operations  1.32 us (1%)
  other arithmetic  1.22 us (1%)
    all_to_all x1, blocking collectives, local(): lax.all_to_all(terms, 'freq', split_axis=0, concat_axis=0, tiled=True)  19.2 us
    all_to_all x1, starting transfers between devices, local(): lax.all_to_all(copies, BLK, split_axis=0, concat_axis=0, tiled=True)  17.8 us
    pallas_call x1, Pallas kernels, local(): pl.pallas_call(first_kernel, out_shape=(jax.ShapeDtypeStruct((2, tx, own)...  16.8 us
    pallas_call x1, Pallas kernels, local(): pl.pallas_call(functools.partial(second_kernel, node_count=count), out_sh...  14.3 us
    all_to_all x1, blocking collectives, local(): lax.all_to_all(part, REDUCE, split_axis=0, concat_axis=0, tiled=True)  13.5 us
    all_to_all x1, waiting for transfers between devices, local(): lax.all_to_all(weighted, GATHER, split_axis=0, concat_axis=0, tiled=True)  10.2 us
    all_to_all x1, waiting for transfers between devices, local(): lax.all_to_all(copies, BLK, split_axis=0, concat_axis=0, tiled=True)  9.56 us
    all_to_all x1, starting transfers between devices, local(): lax.all_to_all(weighted, GATHER, split_axis=0, concat_axis=0, tiled=True)  3.57 us
  transfers between devices with their start and end apart: 2, of which 2 were waited for; matrix products, arithmetic and copies ran while one was open for 3% of the time, Pallas kernels for 0%

profile of v1, /device:TPU:1, one launch (start us, length us, event | category | flops | bytes accessed | tf_op | source)
XLA Modules:
  0.0 115.2 jit_solution(11779203841808779599)
XLA Ops:
  0.6 0.7 convert_element_type.3.own_ref
  1.3 0.0 copy-start.2
  1.3 0.7 broadcast_in_dim.6
  2.0 0.0 copy-done.2
  2.0 17.8 %all-to-all-start = ((bf16[128,3,128]{2,1,0:T(4,128)(2,1)}), bf16[128,3,128]{2,1,0:T(4,128)(2,1)S(1)}, u32[]{:S(2)}, u32[]{:S(2)}) async-start(bf16[128,3,128]{2,1,0:T(4,128)(2,1)} %broadcast_in_dim.6), calls=%async_computation | async-start | bytes 262144 | tf_op jit(solution)/shard_map/all_to_all | solution.py:232
  20.4 0.0 copy-start.3
  20.4 0.6 copy-done.3
  21.1 0.7 copy.8.emitters_ref
  21.8 9.6 %all-to-all-done.places_ref = bf16[128,3,128]{2,1,0:T(4,128)(2,1)S(1)} async-done(((bf16[128,3,128]{2,1,0:T(4,128)(2,1)}), bf16[128,3,128]{2,1,0:T(4,128)(2,1)S(1)}, u32[]{:S(2)}, u32[]{:S(2)}) %all-to-all-start) | async-done | bytes 98336 | tf_op jit(solution)/shard_map/all_to_all | solution.py:232
  31.3 0.0 copy-start.1
  31.4 0.6 copy-done.1
  32.0 16.8 %first_wave.1 = (f32[2,64,128]{2,1,0:T(8,128)}, bf16[16,2,64,128]{3,2,1,0:T(8,128)(2,1)}) custom-call(f32[1]{0:T(128)S(6)} %copy.11.turns_ref, bf16[128,3,128]{2,1,0:T(4,128)(2,1)} %copy-done.1, bf16[3,128]{1,0:T(4,128)(2,1)} %copy-done.2, s32[64,1]{1,0:T(8,128)} %copy.8.emitters_ref, f32[2,128]{1,0:T(2,128)} %admittance_ref.1), custom_call_target="tpu_custom_call" | custom-call | tf_op jit(solution)/shard_map/first_wave/pallas_call | solution.py:235
  48.8 3.6 %all-to-all-start.1 = ((bf16[16,2,64,128]{3,2,1,0:T(8,128)(2,1)}), bf16[16,2,64,128]{3,2,1,0:T(8,128)(2,1)S(1)}, u32[]{:S(2)}, u32[]{:S(2)}) async-start(bf16[16,2,64,128]{3,2,1,0:T(8,128)(2,1)} %get-tuple-element.6), calls=%async_computation.1 | async-start | bytes 1048576 | tf_op jit(solution)/shard_map/all_to_all | solution.py:260
  52.4 1.3 %dynamic-slice_bitcast_fusion.row_places_ref = bf16[8,3,128]{2,1,0:T(4,128)(2,1)} fusion(bf16[4,8,4,3,128]{4,3,2,1,0:T(4,128)(2,1)} %bitcast.9, s32[]{:T(128)S(6)} %select_n.17, s32[]{:T(128)S(6)} %select_n.19), kind=kLoop, calls=%fused_computation | loop fusion | bytes 12296 | tf_op jit(solution)/shard_map/jit(dynamic_index_in_dim)/squeeze | solution.py:256
  53.7 1.3 %constant_dynamic-slice_fusion = bf16[4,1,4,3,128]{4,3,2,1,0:T(4,128)(2,1)} fusion(bf16[4,8,4,3,128]{4,3,2,1,0:T(4,128)(2,1)} %bitcast.10, s32[]{:T(128)S(6)} %select_n.20), kind=kLoop, calls=%fused_computation.1 | loop fusion | bytes 24580 | tf_op jit(solution)/shard_map/jit(dynamic_index_in_dim)/dynamic_slice | solution.py:259
  55.0 10.2 %all-to-all-done.1.source_ref = bf16[16,2,64,128]{3,2,1,0:T(8,128)(2,1)S(1)} async-done(((bf16[16,2,64,128]{3,2,1,0:T(8,128)(2,1)}), bf16[16,2,64,128]{3,2,1,0:T(8,128)(2,1)S(1)}, u32[]{:S(2)}, u32[]{:S(2)}) %all-to-all-start.1) | async-done | bytes 524320 | tf_op jit(solution)/shard_map/all_to_all | solution.py:260
  65.2 0.0 copy-start
  65.2 0.8 copy-done
  66.0 14.3 %second_wave.1 = bf16[8,2,64,128]{3,2,1,0:T(8,128)(2,1)} custom-call(f32[1]{0:T(128)S(6)} %copy.11.turns_ref, bf16[8,3,128]{2,1,0:T(4,128)(2,1)} %dynamic-slice_bitcast_fusion.row_places_ref, bf16[16,3,128]{2,1,0:T(4,128)(2,1)} %bitcast.11, bf16[16,2,64,128]{3,2,1,0:T(8,128)(2,1)} %copy-done), custom_call_target="tpu_custom_call" | custom-call | tf_op jit(solution)/shard_map/second_wave/pallas_call | solution.py:263
  80.3 13.5 %all_to_all.20.parts_ref = bf16[8,2,64,128]{3,2,1,0:T(8,128)(2,1)} all-to-all(bf16[8,2,64,128]{3,2,1,0:T(8,128)(2,1)} %second_wave.1), channel_id=1, replica_groups=mesh['z'=4,'y'=8,'x'=4,'freq'=4] {'y'}, dimensions={0} | all-to-all | bytes 524288 | tf_op jit(solution)/shard_map/all_to_all | solution.py:282
  93.8 1.6 %last_sum.1 = (bf16[1,2,64,128]{3,2,1,0:T(8,128)(2,1)}, f32[4,1,128]{2,1,0:T(1,128)}) custom-call(bf16[8,2,64,128]{3,2,1,0:T(8,128)(2,1)} %all_to_all.20.parts_ref, f32[2,64,128]{2,1,0:T(8,128)} %get-tuple-element.7.first_ref), custom_call_target="tpu_custom_call" | custom-call | tf_op jit(solution)/shard_map/last_sum/pallas_call | solution.py:283
  95.4 19.2 %all_to_all.21 = f32[4,1,128]{2,1,0:T(1,128)S(1)} all-to-all(f32[4,1,128]{2,1,0:T(1,128)} %get-tuple-element.9), channel_id=1, replica_groups=mesh['z'=4,'y'=8,'x'=4,'freq'=4] {'freq'}, dimensions={0} | all-to-all | bytes 4096 | tf_op jit(solution)/shard_map/all_to_all | solution.py:293
  114.6 0.5 reduce_sum.9
Async XLA Ops:
  1.3 0.7 copy-start.2
  2.0 29.3 %all-to-all-start = ((bf16[128,3,128]{2,1,0:T(4,128)(2,1)}), bf16[128,3,128]{2,1,0:T(4,128)(2,1)S(1)}, u32[]{:S(2)}, u32[]{:S(2)}) async-start(bf16[128,3,128]{2,1,0:T(4,128)(2,1)} %broadcast_in_dim.6), calls=%async_computation | async-start | bytes 262144 | tf_op jit(solution)/shard_map/all_to_all | solution.py:232
  20.4 0.7 copy-start.3
  31.3 0.6 copy-start.1
  48.8 16.4 %all-to-all-start.1 = ((bf16[16,2,64,128]{3,2,1,0:T(8,128)(2,1)}), bf16[16,2,64,128]{3,2,1,0:T(8,128)(2,1)S(1)}, u32[]{:S(2)}, u32[]{:S(2)}) async-start(bf16[16,2,64,128]{3,2,1,0:T(8,128)(2,1)} %get-tuple-element.6), calls=%async_computation.1 | async-start | bytes 1048576 | tf_op jit(solution)/shard_map/all_to_all | solution.py:260
  65.2 0.8 copy-start

commit v2 on v1

--- a/solution.py
+++ b/solution.py
@@ -1,3 +1,4 @@
+import functools
 import math
 
 import jax
@@ -84,18 +85,29 @@
     return spread
 
 
-def first_kernel(turns_ref, places_ref, own_ref, emitters_ref, admittance_ref, first_ref, weighted_ref,
-                 cols_ref, rows_ref, d0, d1, g0, g1, acc_ref):
+def start_kernel(wavenumber_ref, own_ref, emitters_ref, admittance_ref, copies_ref, rows_ref, index_ref, side_ref):
+    own = own_ref[...].astype(jnp.bfloat16)
+    copies_ref[...] = jnp.broadcast_to(own[None], copies_ref.shape)
+    rows_ref[...] = row_features(*rows_of(own)).astype(jnp.bfloat16)
+    emitters = jnp.broadcast_to(emitters_ref[...].astype(jnp.float32), (LANES, emitters_ref.shape[1]))
+    index_ref[...] = jnp.transpose(emitters).astype(jnp.int32)
+    turns = wavenumber_ref[...] * (1.0 / (GRID * 2.0 * math.pi))
+    side_ref[...] = jnp.broadcast_to(turns, side_ref.shape)
+    side_ref[1:3] = admittance_ref[...]
+
+
+def first_kernel(side_ref, places_ref, own_rows_ref, index_ref, first_ref, weighted_ref,
+                 rows_ref, d0, d1, g0, g1, acc_ref):
     blocks = places_ref.shape[0]
-    own = own_ref.shape[1]
-    emitters = emitters_ref.shape[0]
+    own = own_rows_ref.shape[0]
+    emitters = index_ref.shape[0]
     width = d0.shape[1]
     per = width // own
     chunks = blocks // per
-    turns = turns_ref[0] * (1.0 / (GRID * 2.0 * math.pi))
-
-    rows_ref[0:own] = row_features(*rows_of(own_ref[...])).astype(jnp.bfloat16)
-    index = jnp.broadcast_to(emitters_ref[...], (emitters, LANES))
+    turns = side_ref[0:1, 0:1]
+
+    rows_ref[0:own] = own_rows_ref[...]
+    index = index_ref[...]
     lane = lax.broadcasted_iota(jnp.int32, (emitters, LANES), 1)
     of_block = jnp.where(lane == index // own, 1.0, 0.0).astype(jnp.bfloat16)
     at_lane = lane == index % own
@@ -144,7 +156,7 @@
     imag = (low[:, 0:own] + top[:, own:]) * scale
     first_ref[0] = real
     first_ref[1] = imag
-    a, b = admittance_ref[0:1, :], admittance_ref[1:2, :]
+    a, b = side_ref[1:2, :], side_ref[2:3, :]
     w_real = (a * real - b * imag).astype(jnp.bfloat16)
     w_imag = (a * imag + b * real).astype(jnp.bfloat16)
     for k in range(weighted_ref.shape[0]):
@@ -152,49 +164,77 @@
         weighted_ref[k, 1] = w_imag
 
 
-def second_kernel(turns_ref, row_places_ref, col_places_ref, source_ref, part_ref,
-                  cols_ref, rows_ref, d0, d1, r0, i0, r1, i1, acc_r, acc_i, *, node_count):
-    groups, _, own = col_places_ref.shape
-    targets = row_places_ref.shape[0]
-    emitters = source_ref.shape[2]
-    width = targets * own
-    turns = turns_ref[0] * (1.0 / (GRID * 2.0 * math.pi))
-    for b in range(targets):
-        cols_ref[:, b * own : (b + 1) * own] = column_features(row_places_ref[b]).astype(jnp.bfloat16)
-    acc_r[...] = jnp.zeros_like(acc_r)
-    acc_i[...] = jnp.zeros_like(acc_i)
+def tile_kernel(side_ref, places_ref, after_ref, tile_ref, cols_ref, d0, d1, t0, t1, sems, *, sizes):
+    nz, ny, nx = sizes
+    own = places_ref.shape[2]
+    width = ny * own
+    iz, iy, ix = (lax.axis_index(a) for a in BLK)
+    turns = side_ref[0:1, 0:1]
+    for b in range(ny):
+        block = (iz * ny + b) * nx + ix
+        cols_ref[:, b * own : (b + 1) * own] = column_features(places_ref[block]).astype(jnp.bfloat16)
 
     def distances(c, d_ref):
-        rows = row_features(*rows_of(col_places_ref[c])).astype(jnp.bfloat16)
+        block = ((c // nx) * ny + iy) * nx + c % nx
+        rows = row_features(*rows_of(places_ref[block])).astype(jnp.bfloat16)
         d_ref[...] = dot(rows[:, 0:FEATURES], cols_ref[...])
 
-    def tile(d_ref, r_ref, i_ref):
+    def tile(d_ref, t_ref):
         for r in range(0, own, 16):
             for w in range(0, width, 512):
                 real, imag = green_parts(d_ref[r : r + 16, w : w + 512], turns)
-                r_ref[r : r + 16, w : w + 512] = real.astype(jnp.bfloat16)
-                i_ref[r : r + 16, w : w + 512] = imag.astype(jnp.bfloat16)
-
-    def gather(c, r_ref, i_ref):
-        lhs = source_ref[c].reshape(2 * emitters, own)
-        acc_r[...] += dot(lhs, r_ref[...])
-        acc_i[...] += dot(lhs, i_ref[...])
+                t_ref[0, r : r + 16, w : w + 512] = real.astype(jnp.bfloat16)
+                t_ref[1, r : r + 16, w : w + 512] = imag.astype(jnp.bfloat16)
+
+    def out(c, t_ref, s):
+        return pltpu.make_async_copy(t_ref, tile_ref.at[c], sems.at[s])
 
     distances(0, d0)
-    r1[...] = jnp.zeros_like(r1)
-    i1[...] = jnp.zeros_like(i1)
 
     def pair(k, carry):
+        @pl.when(k > 0)
+        def _():
+            out(2 * k - 2, t0, 0).wait()
+
         distances(2 * k + 1, d1)
-        tile(d0, r0, i0)
-        gather(jnp.maximum(2 * k - 1, 0), r1, i1)
-        distances(jnp.minimum(2 * k + 2, groups - 1), d0)
-        tile(d1, r1, i1)
-        gather(2 * k, r0, i0)
+        tile(d0, t0)
+        out(2 * k, t0, 0).start()
+
+        @pl.when(k > 0)
+        def _():
+            out(2 * k - 1, t1, 1).wait()
+
+        distances(jnp.minimum(2 * k + 2, nz * nx - 1), d0)
+        tile(d1, t1)
+        out(2 * k + 1, t1, 1).start()
         return carry
 
-    lax.fori_loop(0, groups // 2, pair, 0)
-    gather(groups - 1, r1, i1)
+    lax.fori_loop(0, nz * nx // 2, pair, 0)
+    out(nz * nx - 2, t0, 0).wait()
+    out(nz * nx - 1, t1, 1).wait()
+
+
+def second_kernel(source_ref, tile_ref, part_ref, lhs_ref, all_ref, acc_r, acc_i, sems, *, node_count):
+    groups, _, emitters, own = source_ref.shape
+    targets = part_ref.shape[0]
+    pieces = sems.shape[0]
+    per = groups // pieces
+
+    def bring(p):
+        at = pl.ds(p * per, per)
+        return pltpu.make_async_copy(tile_ref.at[at], all_ref.at[at], sems.at[p])
+
+    for p in range(pieces):
+        bring(p).start()
+    for c in range(groups):
+        lhs_ref[:, c * own : (c + 1) * own] = source_ref[c].reshape(2 * emitters, own)
+    for p in range(pieces):
+        bring(p).wait()
+        lhs = lhs_ref[:, p * per * own : (p + 1) * per * own]
+        for part, acc in ((0, acc_r), (1, acc_i)):
+            rhs = all_ref[p * per : (p + 1) * per, part].reshape(per * own, targets * own)
+            here = dot(lhs, rhs)
+            acc[...] = here if p == 0 else acc[...] + here
     scale = GRID * float(node_count) ** (-0.5)
     for b in range(targets):
         at = slice(b * own, (b + 1) * own)
@@ -215,7 +255,11 @@
 
 
 VMEM = pl.BlockSpec(memory_space=pltpu.VMEM)
-SMEM = pl.BlockSpec(memory_space=pltpu.SMEM)
+HBM = pl.BlockSpec(memory_space=pltpu.HBM)
+
+
+def limit(mib):
+    return pltpu.CompilerParams(vmem_limit_bytes=mib << 20)
 
 
 def local(node_index, emitters, admittance, wavenumbers):
@@ -227,10 +271,21 @@
     tx = emitters.shape[0]
     near, far = lax.axis_size(GATHER), lax.axis_size(REDUCE)
 
-    own_places = node_index.astype(jnp.bfloat16)
-    copies = jnp.broadcast_to(own_places, (blocks, *own_places.shape))
+    f32, bf16 = jnp.float32, jnp.bfloat16
+    copies, own_rows, index, side = pl.pallas_call(
+        start_kernel,
+        out_shape=(
+            jax.ShapeDtypeStruct((blocks, 3, own), bf16),
+            jax.ShapeDtypeStruct((own, LANES), bf16),
+            jax.ShapeDtypeStruct((tx, LANES), jnp.int32),
+            jax.ShapeDtypeStruct((8, own), f32),
+        ),
+        in_specs=[VMEM] * 4,
+        out_specs=(VMEM,) * 4,
+        compiler_params=limit(4),
+        name="start",
+    )(wavenumbers[None], node_index, emitters[None], admittance)
     places = lax.all_to_all(copies, BLK, split_axis=0, concat_axis=0, tiled=True)
-    f32, bf16 = jnp.float32, jnp.bfloat16
     width = 4 * own
     first, weighted = pl.pallas_call(
         first_kernel,
@@ -238,10 +293,9 @@
             jax.ShapeDtypeStruct((2, tx, own), f32),
             jax.ShapeDtypeStruct((near, 2, tx, own), bf16),
         ),
-        in_specs=[SMEM, VMEM, VMEM, VMEM, VMEM],
+        in_specs=[VMEM] * 4,
         out_specs=(VMEM, VMEM),
         scratch_shapes=[
-            pltpu.VMEM((FEATURES, width), bf16),
             pltpu.VMEM((own + tx, LANES), bf16),
             pltpu.VMEM((own + tx, width), f32),
             pltpu.VMEM((own + tx, width), f32),
@@ -249,36 +303,43 @@
             pltpu.VMEM((2 * (own + tx), width), bf16),
             pltpu.VMEM((2 * tx, 2 * own), f32),
         ],
+        compiler_params=limit(8),
         name="first_wave",
-    )(wavenumbers, places, own_places, emitters[:, None], admittance)
-
-    grouped = places.reshape(*sizes, 3, own)
-    row_places = lax.dynamic_index_in_dim(
-        lax.dynamic_index_in_dim(grouped, lax.axis_index("z"), 0, False), lax.axis_index("x"), 1, False
-    )
-    col_places = lax.dynamic_index_in_dim(grouped, lax.axis_index("y"), 1, False).reshape(near, 3, own)
+    )(side, places, own_rows, index)
+
     source = lax.all_to_all(weighted, GATHER, split_axis=0, concat_axis=0, tiled=True)
-    import functools
-
+    tile = pl.pallas_call(
+        functools.partial(tile_kernel, sizes=sizes),
+        out_shape=jax.ShapeDtypeStruct((near, 2, own, far * own), bf16),
+        in_specs=[VMEM, VMEM, pl.BlockSpec(memory_space=pl.ANY)],
+        out_specs=HBM,
+        scratch_shapes=[
+            pltpu.VMEM((FEATURES, far * own), bf16),
+            pltpu.VMEM((own, far * own), f32),
+            pltpu.VMEM((own, far * own), f32),
+            pltpu.VMEM((2, own, far * own), bf16),
+            pltpu.VMEM((2, own, far * own), bf16),
+            pltpu.SemaphoreType.DMA((2,)),
+        ],
+        compiler_params=limit(50),
+        cost_estimate=pl.CostEstimate(flops=10**10, bytes_accessed=1 << 23, transcendentals=1 << 21),
+        name="green_tile",
+    )(side, places, first)
     part = pl.pallas_call(
         functools.partial(second_kernel, node_count=count),
         out_shape=jax.ShapeDtypeStruct((far, 2, tx, own), bf16),
-        in_specs=[SMEM, VMEM, VMEM, VMEM],
+        in_specs=[VMEM, HBM],
         out_specs=VMEM,
         scratch_shapes=[
-            pltpu.VMEM((FEATURES, far * own), bf16),
-            pltpu.VMEM((own, LANES), bf16),
-            pltpu.VMEM((own, far * own), f32),
-            pltpu.VMEM((own, far * own), f32),
-            pltpu.VMEM((own, far * own), bf16),
-            pltpu.VMEM((own, far * own), bf16),
-            pltpu.VMEM((own, far * own), bf16),
-            pltpu.VMEM((own, far * own), bf16),
+            pltpu.VMEM((2 * tx, near * own), bf16),
+            pltpu.VMEM((near, 2, own, far * own), bf16),
             pltpu.VMEM((2 * tx, far * own), f32),
             pltpu.VMEM((2 * tx, far * own), f32),
+            pltpu.SemaphoreType.DMA((4,)),
         ],
+        compiler_params=limit(50),
         name="second_wave",
-    )(wavenumbers, row_places, col_places, source)
+    )(source, tile)
     parts = lax.all_to_all(part, REDUCE, split_axis=0, concat_axis=0, tiled=True)
     second, terms = pl.pallas_call(
         functools.partial(last_kernel, share=1.0 / (lanes * tx)),
@@ -288,6 +349,7 @@
         ),
         in_specs=[VMEM, VMEM],
         out_specs=(VMEM, VMEM),
+        compiler_params=limit(4),
         name="last_sum",
     )(parts, first)
     terms = lax.all_to_all(terms, "freq", split_axis=0, concat_axis=0, tiled=True)

time: 116 us -> 101 us (0.87)
  blocking collectives: 32.7 us -> 59.9 us
  waiting for transfers between devices: 19.8 us -> 0.01 us
  starting transfers between devices: 21.3 us -> 3.57 us
  local copies, waits for them, and re-layouts: 6.1 us -> 2.01 us
    all_to_all x0 -> x1, blocking collectives: none -> 29.1 us  [local(): lax.all_to_all(copies, BLK, split_axis=0, concat_axis=0, tiled=True)]
    all_to_all x1 -> x0, starting transfers between devices: 17.8 us -> none  [local(): lax.all_to_all(copies, BLK, split_axis=0, concat_axis=0, tiled=True)]
    pallas_call x0 -> x2, Pallas kernels: none -> 13 us  [the longest x1 12.9 us: local(): pl.pallas_call(functools.partial(tile_kernel, sizes=sizes), out_shape=jax...]
    pallas_call x1, Pallas kernels: 14.3 us -> 3.96 us  [local(): pl.pallas_call(functools.partial(second_kernel, node_count=count), out_sh...]
    all_to_all x1, waiting for transfers between devices: 10.2 us -> 0.01 us  [local(): lax.all_to_all(weighted, GATHER, split_axis=0, concat_axis=0, tiled=True)]
    all_to_all x1 -> x0, waiting for transfers between devices: 9.56 us -> none  [local(): lax.all_to_all(copies, BLK, split_axis=0, concat_axis=0, tiled=True)]
    all_to_all x1, blocking collectives: 13.5 us -> 11.9 us  [local(): lax.all_to_all(part, REDUCE, split_axis=0, concat_axis=0, tiled=True)]
    broadcast_in_dim x2 -> x0, local copies, waits for them, and re-layouts: 1.4 us -> none  [the longest x1 0.71 us: local(): emitters[:, None]]
  transfers between devices with their start and end apart: 2 -> 1, of which waited for: 2 -> 0; matrix products, arithmetic and copies ran while one was open for 3% -> 0% of each run, Pallas kernels for 0% -> 13%
where the time goes in v2:
time: 101 us
  blocking collectives  59.9 us (59%)
  Pallas kernels  33.4 us (33%)
  starting transfers between devices  3.57 us (4%)
  local copies, waits for them, and re-layouts  2.01 us (2%)
  between operations  1.33 us (1%)
    all_to_all x1, blocking collectives, local(): lax.all_to_all(copies, BLK, split_axis=0, concat_axis=0, tiled=True)  29.1 us
    all_to_all x1, blocking collectives, local(): lax.all_to_all(terms, 'freq', split_axis=0, concat_axis=0, tiled=True)  18.9 us
    pallas_call x1, Pallas kernels, local(): pl.pallas_call(first_kernel, out_shape=(jax.ShapeDtypeStruct((2, tx, own)...  15.8 us
    pallas_call x1, Pallas kernels, local(): pl.pallas_call(functools.partial(tile_kernel, sizes=sizes), out_shape=jax...  12.9 us
    all_to_all x1, blocking collectives, local(): lax.all_to_all(part, REDUCE, split_axis=0, concat_axis=0, tiled=True)  11.9 us
    pallas_call x1, Pallas kernels, local(): pl.pallas_call(functools.partial(second_kernel, node_count=count), out_sh...  3.96 us
    all_to_all x1, starting transfers between devices, local(): lax.all_to_all(weighted, GATHER, split_axis=0, concat_axis=0, tiled=True)  3.57 us
  transfers between devices with their start and end apart: 1, of which 0 were waited for; matrix products, arithmetic and copies ran while one was open for 0% of the time, Pallas kernels for 13%

profile of v2, /device:TPU:1, one launch (start us, length us, event | category | flops | bytes accessed | tf_op | source)
XLA Modules:
  0.0 100.8 jit_solution(5434174858625560860)
XLA Ops:
  1.3 0.0 copy-start
  1.3 0.7 copy-done
  2.0 0.0 copy-start.1
  2.0 0.7 copy-done.1
  2.6 0.0 copy-start.2
  2.6 0.7 copy-done.2
  3.3 0.2 start.1
  3.5 29.1 %all_to_all.20.places_ref = bf16[128,3,128]{2,1,0:T(4,128)(2,1)S(1)} all-to-all(bf16[128,3,128]{2,1,0:T(4,128)(2,1)S(1)} %get-tuple-element.11), channel_id=1, replica_groups=mesh['z'=4,'y'=8,'x'=4,'freq'=4] {'z','y','x'}, dimensions={0} | all-to-all | bytes 196608 | tf_op jit(solution)/shard_map/all_to_all | solution.py:288
  32.6 15.8 %first_wave.1 = (f32[2,64,128]{2,1,0:T(8,128)S(1)}, bf16[16,2,64,128]{3,2,1,0:T(8,128)(2,1)}) custom-call(f32[8,128]{1,0:T(8,128)S(1)} %get-tuple-element.10.side_ref, bf16[128,3,128]{2,1,0:T(4,128)(2,1)S(1)} %all_to_all.20.places_ref, bf16[128,128]{1,0:T(8,128)(2,1)S(1)} %get-tuple-element.12.own_rows_ref, s32[64,128]{1,0:T(8,128)S(1)} %get-tuple-element.13.index_ref), custom_call_target="tpu_custom_call" | custom-call | tf_op jit(solution)/shard_map/first_wave/pallas_call | solution.py:290
  48.4 3.6 %all-to-all-start.1 = ((bf16[16,2,64,128]{3,2,1,0:T(8,128)(2,1)}), bf16[16,2,64,128]{3,2,1,0:T(8,128)(2,1)S(1)}, u32[]{:S(2)}, u32[]{:S(2)}) async-start(bf16[16,2,64,128]{3,2,1,0:T(8,128)(2,1)} %get-tuple-element.14), calls=%async_computation.1 | async-start | bytes 1048576 | tf_op jit(solution)/shard_map/all_to_all | solution.py:310
  52.0 12.9 %green_tile.1.tile_ref = bf16[16,2,128,1024]{3,2,1,0:T(8,128)(2,1)} custom-call(f32[8,128]{1,0:T(8,128)S(1)} %get-tuple-element.10.side_ref, bf16[128,3,128]{2,1,0:T(4,128)(2,1)S(1)} %all_to_all.20.places_ref, f32[2,64,128]{2,1,0:T(8,128)S(1)} %get-tuple-element.15.after_ref.first_ref), custom_call_target="tpu_custom_call" | custom-call | flops 10000000000 | bytes 8388608 | tf_op jit(solution)/shard_map/green_tile/pallas_call | solution.py:311
  64.9 0.0 all-to-all-done.1.source_ref
  64.9 4.0 %second_wave.1 = bf16[8,2,64,128]{3,2,1,0:T(8,128)(2,1)S(1)} custom-call(bf16[16,2,64,128]{3,2,1,0:T(8,128)(2,1)S(1)} %all-to-all-done.1.source_ref, bf16[16,2,128,1024]{3,2,1,0:T(8,128)(2,1)} %green_tile.1.tile_ref), custom_call_target="tpu_custom_call" | custom-call | tf_op jit(solution)/shard_map/second_wave/pallas_call | solution.py:328
  68.8 11.9 %all_to_all.21.parts_ref = bf16[8,2,64,128]{3,2,1,0:T(8,128)(2,1)S(1)} all-to-all(bf16[8,2,64,128]{3,2,1,0:T(8,128)(2,1)S(1)} %second_wave.1), channel_id=1, replica_groups=mesh['z'=4,'y'=8,'x'=4,'freq'=4] {'y'}, dimensions={0} | all-to-all | bytes 524288 | tf_op jit(solution)/shard_map/all_to_all | solution.py:343
  80.8 0.7 last_sum.1
  81.4 18.9 %all_to_all.22 = f32[4,1,128]{2,1,0:T(1,128)S(1)} all-to-all(f32[4,1,128]{2,1,0:T(1,128)S(1)} %get-tuple-element.17), channel_id=1, replica_groups=mesh['z'=4,'y'=8,'x'=4,'freq'=4] {'freq'}, dimensions={0} | all-to-all | bytes 4096 | tf_op jit(solution)/shard_map/all_to_all | solution.py:355
  100.3 0.5 reduce_sum.9
Async XLA Ops:
  1.3 0.7 copy-start
  2.0 0.7 copy-start.1
  2.6 0.7 copy-start.2
  48.4 16.5 %all-to-all-start.1 = ((bf16[16,2,64,128]{3,2,1,0:T(8,128)(2,1)}), bf16[16,2,64,128]{3,2,1,0:T(8,128)(2,1)S(1)}, u32[]{:S(2)}, u32[]{:S(2)}) async-start(bf16[16,2,64,128]{3,2,1,0:T(8,128)(2,1)} %get-tuple-element.14), calls=%async_computation.1 | async-start | bytes 1048576 | tf_op jit(solution)/shard_map/all_to_all | solution.py:310

commit v3 on v2

--- a/solution.py
+++ b/solution.py
@@ -10,9 +10,9 @@
 from jax.sharding import PartitionSpec as P
 
 GRID = 64
-BLK = ("z", "y", "x")
-GATHER = ("z", "x")
-REDUCE = "y"
+BLK = ("zs", "za", "y", "x")
+GATHER = ("zs", "y")
+REDUCE = ("za", "x")
 LANES = 128
 FEATURES = 16
 SOFT = 0.0025 * GRID * GRID
@@ -41,21 +41,23 @@
     return inv - q * half_sin, q * half_cos
 
 
-def centred(places):
-    return places.astype(jnp.float32) - 32.0
-
-
-def column_features(places):
-    p = centred(places)
+def split_norm(p):
     n = jnp.sum(p * p, axis=0, keepdims=True)
     high = ((n * (1 / 64) + MAGIC) - MAGIC) * 64.0
-    low = n - high
-    one = jnp.ones_like(n)
-    zero = jnp.zeros((FEATURES - 7, n.shape[1]), jnp.float32)
+    return high, n - high
+
+
+def features(places, target):
+    p = places.astype(jnp.float32) - 32.0
+    high, low = split_norm(p)
+    one = jnp.ones_like(high)
+    zero = jnp.zeros((FEATURES - 7, p.shape[1]), jnp.float32)
+    if target:
+        return jnp.concatenate([p, high, low, one, one, zero], axis=0)
     return jnp.concatenate([p * -2.0, one, one, high, low, zero], axis=0)
 
 
-def row_features(x, y, z):
+def spread_features(x, y, z):
     lane = lax.broadcasted_iota(jnp.int32, x.shape, 1)
     x, y, z = x - 32.0, y - 32.0, z - 32.0
     n = x * x + y * y + z * z
@@ -73,40 +75,26 @@
     return lax.dot_general(a, b, (contract, ((), ())), preferred_element_type=jnp.float32)
 
 
-NT = ((1,), (1,))
-
-
-def rows_of(places):
-    count = places.shape[1]
-    spread = []
-    for d in range(3):
-        line = jnp.broadcast_to(places[d : d + 1, :].astype(jnp.float32), (LANES, count))
-        spread.append(jnp.transpose(line))
-    return spread
-
-
-def start_kernel(wavenumber_ref, own_ref, emitters_ref, admittance_ref, copies_ref, rows_ref, index_ref, side_ref):
-    own = own_ref[...].astype(jnp.bfloat16)
-    copies_ref[...] = jnp.broadcast_to(own[None], copies_ref.shape)
-    rows_ref[...] = row_features(*rows_of(own)).astype(jnp.bfloat16)
+def start_kernel(wavenumber_ref, node_ref, emitters_ref, admittance_ref, own_ref, index_ref, side_ref):
+    own_ref[...] = features(node_ref[...], True).astype(jnp.bfloat16)
     emitters = jnp.broadcast_to(emitters_ref[...].astype(jnp.float32), (LANES, emitters_ref.shape[1]))
     index_ref[...] = jnp.transpose(emitters).astype(jnp.int32)
-    turns = wavenumber_ref[...] * (1.0 / (GRID * 2.0 * math.pi))
-    side_ref[...] = jnp.broadcast_to(turns, side_ref.shape)
-    side_ref[1:3] = admittance_ref[...]
-
-
-def first_kernel(side_ref, places_ref, own_rows_ref, index_ref, first_ref, weighted_ref,
+    side_ref[0:2] = admittance_ref[...]
+    turns = wavenumber_ref[0] * (1.0 / (GRID * 2.0 * math.pi))
+    side_ref[2:8] = jnp.full((6, side_ref.shape[1]), turns, jnp.float32)
+
+
+def first_kernel(side_ref, places_ref, own_ref, index_ref, first_ref, weighted_ref,
                  rows_ref, d0, d1, g0, g1, acc_ref):
     blocks = places_ref.shape[0]
-    own = own_rows_ref.shape[0]
+    own = own_ref.shape[1]
     emitters = index_ref.shape[0]
     width = d0.shape[1]
     per = width // own
     chunks = blocks // per
-    turns = side_ref[0:1, 0:1]
-
-    rows_ref[0:own] = own_rows_ref[...]
+    turns = side_ref[6:7, 0:1]
+
+    rows_ref[0:own, 0:FEATURES] = jnp.transpose(own_ref[...].astype(jnp.float32)).astype(jnp.bfloat16)
     index = index_ref[...]
     lane = lax.broadcasted_iota(jnp.int32, (emitters, LANES), 1)
     of_block = jnp.where(lane == index // own, 1.0, 0.0).astype(jnp.bfloat16)
@@ -116,25 +104,26 @@
     for d in range(3):
         line = dot(of_block, places_ref[:, d, :])
         found.append(dot(jnp.where(at_lane, line, 0.0).astype(jnp.bfloat16), every))
-    rows_ref[own : own + emitters] = row_features(*found).astype(jnp.bfloat16)
+    rows_ref[own : own + emitters] = spread_features(*found).astype(jnp.bfloat16)
 
     acc_ref[...] = jnp.zeros_like(acc_ref)
 
     def distances(chunk, d_ref):
         for b in range(per):
-            cols = column_features(places_ref[chunk * per + b]).astype(jnp.bfloat16)
-            d_ref[:, b * own : (b + 1) * own] = dot(rows_ref[:, 0:FEATURES], cols)
+            psi = features(places_ref[chunk * per + b], False).astype(jnp.bfloat16)
+            d_ref[:, b * own : (b + 1) * own] = dot(rows_ref[:, 0:FEATURES], psi)
 
     def tile(d_ref, g_ref):
         for r in range(0, own + emitters, 16):
-            real, imag = green_parts(d_ref[r : r + 16, :], turns)
             at = r if r < own else r + own
             step = own if r < own else emitters
-            g_ref[at : at + 16, :] = real.astype(jnp.bfloat16)
-            g_ref[at + step : at + step + 16, :] = imag.astype(jnp.bfloat16)
+            for w in range(0, width, 512):
+                real, imag = green_parts(d_ref[r : r + 16, w : w + 512], turns)
+                g_ref[at : at + 16, w : w + 512] = real.astype(jnp.bfloat16)
+                g_ref[at + step : at + step + 16, w : w + 512] = imag.astype(jnp.bfloat16)
 
     def gather(g_ref):
-        acc_ref[...] += dot(g_ref[2 * own :, :], g_ref[0 : 2 * own, :], NT)
+        acc_ref[...] += dot(g_ref[2 * own :, :], g_ref[0 : 2 * own, :], ((1,), (1,)))
 
     distances(0, d0)
     g1[...] = jnp.zeros_like(g1)
@@ -156,7 +145,7 @@
     imag = (low[:, 0:own] + top[:, own:]) * scale
     first_ref[0] = real
     first_ref[1] = imag
-    a, b = side_ref[1:2, :], side_ref[2:3, :]
+    a, b = side_ref[0:1, :], side_ref[1:2, :]
     w_real = (a * real - b * imag).astype(jnp.bfloat16)
     w_imag = (a * imag + b * real).astype(jnp.bfloat16)
     for k in range(weighted_ref.shape[0]):
@@ -164,20 +153,35 @@
         weighted_ref[k, 1] = w_imag
 
 
+def block_at(where, sizes):
+    place = 0
+    for a in BLK:
+        place = place * sizes[a] + where[a]
+    return place
+
+
+def unravel(k, axes, sizes):
+    where = {}
+    for a in reversed(axes):
+        where[a] = k % sizes[a]
+        k = k // sizes[a]
+    return where
+
+
 def tile_kernel(side_ref, places_ref, after_ref, tile_ref, cols_ref, d0, d1, t0, t1, sems, *, sizes):
-    nz, ny, nx = sizes
+    here = {a: lax.axis_index(a) for a in BLK}
     own = places_ref.shape[2]
-    width = ny * own
-    iz, iy, ix = (lax.axis_index(a) for a in BLK)
-    turns = side_ref[0:1, 0:1]
-    for b in range(ny):
-        block = (iz * ny + b) * nx + ix
-        cols_ref[:, b * own : (b + 1) * own] = column_features(places_ref[block]).astype(jnp.bfloat16)
+    groups = tile_ref.shape[0]
+    width = tile_ref.shape[3]
+    turns = side_ref[6:7, 0:1]
+    for b in range(width // own):
+        block = block_at({**here, **unravel(b, REDUCE, sizes)}, sizes)
+        cols_ref[:, b * own : (b + 1) * own] = features(places_ref[block], True).astype(jnp.bfloat16)
 
     def distances(c, d_ref):
-        block = ((c // nx) * ny + iy) * nx + c % nx
-        rows = row_features(*rows_of(places_ref[block])).astype(jnp.bfloat16)
-        d_ref[...] = dot(rows[:, 0:FEATURES], cols_ref[...])
+        block = block_at({**here, **unravel(c, GATHER, sizes)}, sizes)
+        psi = jnp.transpose(features(places_ref[block], False)).astype(jnp.bfloat16)
+        d_ref[...] = dot(psi, cols_ref[...])
 
     def tile(d_ref, t_ref):
         for r in range(0, own, 16):
@@ -187,31 +191,42 @@
                 t_ref[1, r : r + 16, w : w + 512] = imag.astype(jnp.bfloat16)
 
     def out(c, t_ref, s):
-        return pltpu.make_async_copy(t_ref, tile_ref.at[c], sems.at[s])
+        half = own // 2
+        return [
+            pltpu.make_async_copy(
+                t_ref.at[p, h * half : (h + 1) * half], tile_ref.at[c, p, h * half : (h + 1) * half], sems.at[s, p, h]
+            )
+            for p in range(2)
+            for h in range(2)
+        ]
 
     distances(0, d0)
 
     def pair(k, carry):
         @pl.when(k > 0)
         def _():
-            out(2 * k - 2, t0, 0).wait()
+            for copy in out(2 * k - 2, t0, 0):
+                copy.wait()
 
         distances(2 * k + 1, d1)
         tile(d0, t0)
-        out(2 * k, t0, 0).start()
+        for copy in out(2 * k, t0, 0):
+            copy.start()
 
         @pl.when(k > 0)
         def _():
-            out(2 * k - 1, t1, 1).wait()
-
-        distances(jnp.minimum(2 * k + 2, nz * nx - 1), d0)
+            for copy in out(2 * k - 1, t1, 1):
+                copy.wait()
+
+        distances(jnp.minimum(2 * k + 2, groups - 1), d0)
         tile(d1, t1)
-        out(2 * k + 1, t1, 1).start()
+        for copy in out(2 * k + 1, t1, 1):
+            copy.start()
         return carry
 
-    lax.fori_loop(0, nz * nx // 2, pair, 0)
-    out(nz * nx - 2, t0, 0).wait()
-    out(nz * nx - 1, t1, 1).wait()
+    lax.fori_loop(0, groups // 2, pair, 0)
+    for copy in out(groups - 2, t0, 0) + out(groups - 1, t1, 1):
+        copy.wait()
 
 
 def second_kernel(source_ref, tile_ref, part_ref, lhs_ref, all_ref, acc_r, acc_i, sems, *, node_count):
@@ -256,6 +271,7 @@
 
 VMEM = pl.BlockSpec(memory_space=pltpu.VMEM)
 HBM = pl.BlockSpec(memory_space=pltpu.HBM)
+SMEM = pl.BlockSpec(memory_space=pltpu.SMEM)
 
 
 def limit(mib):
@@ -263,8 +279,8 @@
 
 
 def local(node_index, emitters, admittance, wavenumbers):
-    sizes = [lax.axis_size(a) for a in BLK]
-    blocks = sizes[0] * sizes[1] * sizes[2]
+    sizes = {a: lax.axis_size(a) for a in BLK}
+    blocks = math.prod(sizes.values())
     lanes = lax.axis_size("freq")
     own = node_index.shape[1]
     count = blocks * own
@@ -272,21 +288,21 @@
     near, far = lax.axis_size(GATHER), lax.axis_size(REDUCE)
 
     f32, bf16 = jnp.float32, jnp.bfloat16
-    copies, own_rows, index, side = pl.pallas_call(
+    copies = jnp.broadcast_to(node_index.astype(bf16), (blocks, *node_index.shape))
+    places = lax.all_to_all(copies, BLK, split_axis=0, concat_axis=0, tiled=True)
+    own_features, index, side = pl.pallas_call(
         start_kernel,
         out_shape=(
-            jax.ShapeDtypeStruct((blocks, 3, own), bf16),
-            jax.ShapeDtypeStruct((own, LANES), bf16),
+            jax.ShapeDtypeStruct((FEATURES, own), bf16),
             jax.ShapeDtypeStruct((tx, LANES), jnp.int32),
             jax.ShapeDtypeStruct((8, own), f32),
         ),
-        in_specs=[VMEM] * 4,
-        out_specs=(VMEM,) * 4,
+        in_specs=[SMEM, VMEM, VMEM, VMEM],
+        out_specs=(VMEM,) * 3,
         compiler_params=limit(4),
         name="start",
-    )(wavenumbers[None], node_index, emitters[None], admittance)
-    places = lax.all_to_all(copies, BLK, split_axis=0, concat_axis=0, tiled=True)
-    width = 4 * own
+    )(wavenumbers, node_index, emitters[None], admittance)
+    width = 16 * own
     first, weighted = pl.pallas_call(
         first_kernel,
         out_shape=(
@@ -303,9 +319,9 @@
             pltpu.VMEM((2 * (own + tx), width), bf16),
             pltpu.VMEM((2 * tx, 2 * own), f32),
         ],
-        compiler_params=limit(8),
+        compiler_params=limit(12),
         name="first_wave",
-    )(side, places, own_rows, index)
+    )(side, places, own_features, index)
 
     source = lax.all_to_all(weighted, GATHER, split_axis=0, concat_axis=0, tiled=True)
     tile = pl.pallas_call(
@@ -319,7 +335,7 @@
             pltpu.VMEM((own, far * own), f32),
             pltpu.VMEM((2, own, far * own), bf16),
             pltpu.VMEM((2, own, far * own), bf16),
-            pltpu.SemaphoreType.DMA((2,)),
+            pltpu.SemaphoreType.DMA((2, 2, 2)),
         ],
         compiler_params=limit(50),
         cost_estimate=pl.CostEstimate(flops=10**10, bytes_accessed=1 << 23, transcendentals=1 << 21),
@@ -335,7 +351,7 @@
             pltpu.VMEM((near, 2, own, far * own), bf16),
             pltpu.VMEM((2 * tx, far * own), f32),
             pltpu.VMEM((2 * tx, far * own), f32),
-            pltpu.SemaphoreType.DMA((4,)),
+            pltpu.SemaphoreType.DMA((8,)),
         ],
         compiler_params=limit(50),
         name="second_wave",
@@ -357,7 +373,7 @@
 
 
 def solution(mesh):
-    split = Mesh(mesh.devices.reshape(4, 8, 4, mesh.shape["freq"]), ("z", "y", "x", "freq"))
+    split = Mesh(mesh.devices.reshape(2, 2, 8, 4, mesh.shape["freq"]), (*BLK, "freq"))
     in_specs = (P(None, BLK), P(), P(None, BLK), P("freq"))
     out_specs = (P("freq", None, None, BLK), P(BLK))
     return jax.shard_map(local, mesh=split, in_specs=in_specs, out_specs=out_specs, check_vma=False)

time: 101 us -> 96.3 us (0.953)
  blocking collectives: 59.9 us -> 27 us
  starting transfers between devices: 3.57 us -> 21.3 us
  waiting for transfers between devices: 0.01 us -> 10 us
  Pallas kernels: 33.4 us -> 32.2 us
    all_to_all x1 -> x0, blocking collectives: 29.1 us -> none  [local(): lax.all_to_all(copies, BLK, split_axis=0, concat_axis=0, tiled=True)]
    all_to_all x0 -> x1, starting transfers between devices: none -> 17.8 us  [local(): lax.all_to_all(copies, BLK, split_axis=0, concat_axis=0, tiled=True)]
    all_to_all x0 -> x1, waiting for transfers between devices: none -> 8.82 us  [local(): lax.all_to_all(copies, BLK, split_axis=0, concat_axis=0, tiled=True)]
    all_to_all x1, blocking collectives: 11.9 us -> 8.49 us  [local(): lax.all_to_all(part, REDUCE, split_axis=0, concat_axis=0, tiled=True)]
    all_to_all x1, waiting for transfers between devices: 0.01 us -> 1.21 us  [local(): lax.all_to_all(weighted, GATHER, split_axis=0, concat_axis=0, tiled=True)]
  transfers between devices with their start and end apart: 1 -> 2, of which waited for: 0 -> 2; matrix products, arithmetic and copies ran while one was open for 0% -> 0% of each run, Pallas kernels for 13% -> 13%
where the time goes in v3:
time: 96.3 us; the launch traced here: 95.9 us
  Pallas kernels  32.2 us (33%)
  blocking collectives  27 us (28%)
  starting transfers between devices  21.3 us (22%)
  waiting for transfers between devices  10 us (10%)
  local copies, waits for them, and re-layouts  2.7 us (3%)
  between operations  1.33 us (1%)
  other arithmetic  1.22 us (1%)
    all_to_all x1, blocking collectives, local(): lax.all_to_all(terms, 'freq', split_axis=0, concat_axis=0, tiled=True)  18.5 us
    all_to_all x1, starting transfers between devices, local(): lax.all_to_all(copies, BLK, split_axis=0, concat_axis=0, tiled=True)  17.8 us
    pallas_call x1, Pallas kernels, local(): pl.pallas_call(first_kernel, out_shape=(jax.ShapeDtypeStruct((2, tx, own)...  15 us
    pallas_call x1, Pallas kernels, local(): pl.pallas_call(functools.partial(tile_kernel, sizes=sizes), out_shape=jax...  12.7 us
    all_to_all x1, waiting for transfers between devices, local(): lax.all_to_all(copies, BLK, split_axis=0, concat_axis=0, tiled=True)  8.82 us
    all_to_all x1, blocking collectives, local(): lax.all_to_all(part, REDUCE, split_axis=0, concat_axis=0, tiled=True)  8.49 us
    pallas_call x1, Pallas kernels, local(): pl.pallas_call(functools.partial(second_kernel, node_count=count), out_sh...  3.79 us
    all_to_all x1, starting transfers between devices, local(): lax.all_to_all(weighted, GATHER, split_axis=0, concat_axis=0, tiled=True)  3.57 us
  transfers between devices with their start and end apart: 2, of which 2 were waited for; matrix products, arithmetic and copies ran while one was open for 0% of the time, Pallas kernels for 13%

profile of v3, /device:TPU:1, one launch (start us, length us, event | category | flops | bytes accessed | tf_op | source)
XLA Modules:
  0.0 95.9 jit_solution(9973317984526977374)
XLA Ops:
  0.6 0.7 convert_element_type.3
  1.3 0.7 broadcast_in_dim.7
  2.0 17.8 %all-to-all-start = ((bf16[128,3,128]{2,1,0:T(4,128)(2,1)}), bf16[128,3,128]{2,1,0:T(4,128)(2,1)S(1)}, u32[]{:S(2)}, u32[]{:S(2)}) async-start(bf16[128,3,128]{2,1,0:T(4,128)(2,1)} %broadcast_in_dim.7), calls=%async_computation | async-start | bytes 262144 | tf_op jit(solution)/shard_map/all_to_all | solution.py:292
  20.4 0.0 copy-start
  20.4 0.7 copy-done
  21.1 0.0 copy-start.1
  21.1 0.7 copy-done.1
  21.8 0.0 copy-start.2
  21.8 0.7 copy-done.2
  22.4 0.1 start.1
  22.5 8.8 %all-to-all-done.places_ref = bf16[128,3,128]{2,1,0:T(4,128)(2,1)S(1)} async-done(((bf16[128,3,128]{2,1,0:T(4,128)(2,1)}), bf16[128,3,128]{2,1,0:T(4,128)(2,1)S(1)}, u32[]{:S(2)}, u32[]{:S(2)}) %all-to-all-start) | async-done | bytes 98336 | tf_op jit(solution)/shard_map/all_to_all | solution.py:292
  31.3 15.0 %first_wave.1 = (f32[2,64,128]{2,1,0:T(8,128)S(1)}, bf16[16,2,64,128]{3,2,1,0:T(8,128)(2,1)}) custom-call(f32[8,128]{1,0:T(8,128)S(1)} %get-tuple-element.9.side_ref, bf16[128,3,128]{2,1,0:T(4,128)(2,1)S(1)} %all-to-all-done.places_ref, bf16[16,128]{1,0:T(8,128)(2,1)S(1)} %get-tuple-element.10.own_ref, s32[64,128]{1,0:T(8,128)S(1)} %get-tuple-element.11.index_ref), custom_call_target="tpu_custom_call" | custom-call | tf_op jit(solution)/shard_map/first_wave/pallas_call | solution.py:306
  46.4 3.6 %all-to-all-start.1 = ((bf16[16,2,64,128]{3,2,1,0:T(8,128)(2,1)}), bf16[16,2,64,128]{3,2,1,0:T(8,128)(2,1)S(1)}, u32[]{:S(2)}, u32[]{:S(2)}) async-start(bf16[16,2,64,128]{3,2,1,0:T(8,128)(2,1)} %get-tuple-element.12), calls=%async_computation.1 | async-start | bytes 1048576 | tf_op jit(solution)/shard_map/all_to_all | solution.py:326
  49.9 12.7 %green_tile.1.tile_ref = bf16[16,2,128,1024]{3,2,1,0:T(8,128)(2,1)} custom-call(f32[8,128]{1,0:T(8,128)S(1)} %get-tuple-element.9.side_ref, bf16[128,3,128]{2,1,0:T(4,128)(2,1)S(1)} %all-to-all-done.places_ref, f32[2,64,128]{2,1,0:T(8,128)S(1)} %get-tuple-element.13.after_ref.first_ref), custom_call_target="tpu_custom_call" | custom-call | flops 10000000000 | bytes 8388608 | tf_op jit(solution)/shard_map/green_tile/pallas_call | solution.py:327
  62.7 1.2 %all-to-all-done.1.source_ref = bf16[16,2,64,128]{3,2,1,0:T(8,128)(2,1)S(1)} async-done(((bf16[16,2,64,128]{3,2,1,0:T(8,128)(2,1)}), bf16[16,2,64,128]{3,2,1,0:T(8,128)(2,1)S(1)}, u32[]{:S(2)}, u32[]{:S(2)}) %all-to-all-start.1) | async-done | bytes 524320 | tf_op jit(solution)/shard_map/all_to_all | solution.py:326
  63.9 3.8 %second_wave.1 = bf16[8,2,64,128]{3,2,1,0:T(8,128)(2,1)S(1)} custom-call(bf16[16,2,64,128]{3,2,1,0:T(8,128)(2,1)S(1)} %all-to-all-done.1.source_ref, bf16[16,2,128,1024]{3,2,1,0:T(8,128)(2,1)} %green_tile.1.tile_ref), custom_call_target="tpu_custom_call" | custom-call | tf_op jit(solution)/shard_map/second_wave/pallas_call | solution.py:344
  67.7 8.5 %all_to_all.20.parts_ref = bf16[8,2,64,128]{3,2,1,0:T(8,128)(2,1)S(1)} all-to-all(bf16[8,2,64,128]{3,2,1,0:T(8,128)(2,1)S(1)} %second_wave.1), channel_id=1, replica_groups=mesh['zs'=2,'za'=2,'y'=8,'x'=4,'freq'=4] {'za','x'}, dimensions={0} | all-to-all | bytes 524288 | tf_op jit(solution)/shard_map/all_to_all | solution.py:359
  76.1 0.7 last_sum.1
  76.8 18.5 %all_to_all.21 = f32[4,1,128]{2,1,0:T(1,128)S(1)} all-to-all(f32[4,1,128]{2,1,0:T(1,128)S(1)} %get-tuple-element.15), channel_id=1, replica_groups=mesh['zs'=2,'za'=2,'y'=8,'x'=4,'freq'=4] {'freq'}, dimensions={0} | all-to-all | bytes 4096 | tf_op jit(solution)/shard_map/all_to_all | solution.py:371
  95.3 0.5 reduce_sum.9
Async XLA Ops:
  2.0 29.3 %all-to-all-start = ((bf16[128,3,128]{2,1,0:T(4,128)(2,1)}), bf16[128,3,128]{2,1,0:T(4,128)(2,1)S(1)}, u32[]{:S(2)}, u32[]{:S(2)}) async-start(bf16[128,3,128]{2,1,0:T(4,128)(2,1)} %broadcast_in_dim.7), calls=%async_computation | async-start | bytes 262144 | tf_op jit(solution)/shard_map/all_to_all | solution.py:292
  20.4 0.7 copy-start
  21.1 0.7 copy-start.1
  21.8 0.7 copy-start.2
  46.4 17.5 %all-to-all-start.1 = ((bf16[16,2,64,128]{3,2,1,0:T(8,128)(2,1)}), bf16[16,2,64,128]{3,2,1,0:T(8,128)(2,1)S(1)}, u32[]{:S(2)}, u32[]{:S(2)}) async-start(bf16[16,2,64,128]{3,2,1,0:T(8,128)(2,1)} %get-tuple-element.12), calls=%async_computation.1 | async-start | bytes 1048576 | tf_op jit(solution)/shard_map/all_to_all | solution.py:326

commit v4 on v3

--- a/solution.py
+++ b/solution.py
@@ -17,6 +17,7 @@
 FEATURES = 16
 SOFT = 0.0025 * GRID * GRID
 MAGIC = 12582912.0
+KEPT = 6
 ROOT2 = math.sqrt(2.0)
 SIN_POLY = [ROOT2 * c for c in (3.1415820221197075, -5.167142794757069, 2.541899010399708, -0.554636148527055)]
 COS_POLY = [ROOT2 * c for c in (0.9999933001981278, -4.933938170377516, 4.04128504935244, -1.2221298133692595)]
@@ -73,6 +74,11 @@
 
 def dot(a, b, contract=((1,), (0,))):
     return lax.dot_general(a, b, (contract, ((), ())), preferred_element_type=jnp.float32)
+
+
+def copies_kernel(node_ref, copies_ref):
+    places = node_ref[...].astype(jnp.float32).astype(jnp.bfloat16)
+    copies_ref[...] = jnp.broadcast_to(places[None], copies_ref.shape)
 
 
 def start_kernel(wavenumber_ref, node_ref, emitters_ref, admittance_ref, own_ref, index_ref, side_ref):
@@ -168,10 +174,11 @@
     return where
 
 
-def tile_kernel(side_ref, places_ref, after_ref, tile_ref, cols_ref, d0, d1, t0, t1, sems, *, sizes):
+def tile_kernel(side_ref, places_ref, after_ref, tile_ref, near_ref, cols_ref, d0, d1, t0, t1, sems, *, sizes):
     here = {a: lax.axis_index(a) for a in BLK}
     own = places_ref.shape[2]
-    groups = tile_ref.shape[0]
+    far = tile_ref.shape[0]
+    groups = far + near_ref.shape[0]
     width = tile_ref.shape[3]
     turns = side_ref[6:7, 0:1]
     for b in range(width // own):
@@ -183,12 +190,24 @@
         psi = jnp.transpose(features(places_ref[block], False)).astype(jnp.bfloat16)
         d_ref[...] = dot(psi, cols_ref[...])
 
-    def tile(d_ref, t_ref):
+    def tile(d_ref, store):
         for r in range(0, own, 16):
             for w in range(0, width, 512):
                 real, imag = green_parts(d_ref[r : r + 16, w : w + 512], turns)
-                t_ref[0, r : r + 16, w : w + 512] = real.astype(jnp.bfloat16)
-                t_ref[1, r : r + 16, w : w + 512] = imag.astype(jnp.bfloat16)
+                store(0, r, w, real.astype(jnp.bfloat16))
+                store(1, r, w, imag.astype(jnp.bfloat16))
+
+    def into(t_ref):
+        def store(p, r, w, value):
+            t_ref[p, r : r + 16, w : w + 512] = value
+
+        return store
+
+    def kept(c):
+        def store(p, r, w, value):
+            near_ref[c, p, r : r + 16, w : w + 512] = value
+
+        return store
 
     def out(c, t_ref, s):
         half = own // 2
@@ -209,7 +228,7 @@
                 copy.wait()
 
         distances(2 * k + 1, d1)
-        tile(d0, t0)
+        tile(d0, into(t0))
         for copy in out(2 * k, t0, 0):
             copy.start()
 
@@ -219,37 +238,47 @@
                 copy.wait()
 
         distances(jnp.minimum(2 * k + 2, groups - 1), d0)
-        tile(d1, t1)
+        tile(d1, into(t1))
         for copy in out(2 * k + 1, t1, 1):
             copy.start()
         return carry
 
-    lax.fori_loop(0, groups // 2, pair, 0)
-    for copy in out(groups - 2, t0, 0) + out(groups - 1, t1, 1):
+    lax.fori_loop(0, far // 2, pair, 0)
+
+    def last(k, carry):
+        distances(far + 2 * k + 1, d1)
+        tile(d0, kept(2 * k))
+        distances(jnp.minimum(far + 2 * k + 2, groups - 1), d0)
+        tile(d1, kept(2 * k + 1))
+        return carry
+
+    lax.fori_loop(0, (groups - far) // 2, last, 0)
+    for copy in out(far - 2, t0, 0) + out(far - 1, t1, 1):
         copy.wait()
 
 
-def second_kernel(source_ref, tile_ref, part_ref, lhs_ref, all_ref, acc_r, acc_i, sems, *, node_count):
+def second_kernel(source_ref, tile_ref, near_ref, part_ref, lhs_ref, all_ref, acc_r, acc_i, sems, *, node_count):
     groups, _, emitters, own = source_ref.shape
     targets = part_ref.shape[0]
-    pieces = sems.shape[0]
-    per = groups // pieces
+    far = tile_ref.shape[0]
+    per = far // sems.shape[0]
 
     def bring(p):
         at = pl.ds(p * per, per)
         return pltpu.make_async_copy(tile_ref.at[at], all_ref.at[at], sems.at[p])
 
-    for p in range(pieces):
+    for p in range(far // per):
         bring(p).start()
     for c in range(groups):
         lhs_ref[:, c * own : (c + 1) * own] = source_ref[c].reshape(2 * emitters, own)
-    for p in range(pieces):
-        bring(p).wait()
-        lhs = lhs_ref[:, p * per * own : (p + 1) * per * own]
+    for begin in [*range(far, groups, per), *range(0, far, per)]:
+        if begin < far:
+            bring(begin // per).wait()
+        lhs = lhs_ref[:, begin * own : (begin + per) * own]
         for part, acc in ((0, acc_r), (1, acc_i)):
-            rhs = all_ref[p * per : (p + 1) * per, part].reshape(per * own, targets * own)
-            here = dot(lhs, rhs)
-            acc[...] = here if p == 0 else acc[...] + here
+            held = all_ref[begin : begin + per] if begin < far else near_ref[begin - far : begin - far + per]
+            here = dot(lhs, held[:, part].reshape(per * own, targets * own))
+            acc[...] = here if begin == far else acc[...] + here
     scale = GRID * float(node_count) ** (-0.5)
     for b in range(targets):
         at = slice(b * own, (b + 1) * own)
@@ -288,7 +317,14 @@
     near, far = lax.axis_size(GATHER), lax.axis_size(REDUCE)
 
     f32, bf16 = jnp.float32, jnp.bfloat16
-    copies = jnp.broadcast_to(node_index.astype(bf16), (blocks, *node_index.shape))
+    copies = pl.pallas_call(
+        copies_kernel,
+        out_shape=jax.ShapeDtypeStruct((blocks, *node_index.shape), bf16),
+        in_specs=[VMEM],
+        out_specs=VMEM,
+        compiler_params=limit(60),
+        name="copies",
+    )(node_index)
     places = lax.all_to_all(copies, BLK, split_axis=0, concat_axis=0, tiled=True)
     own_features, index, side = pl.pallas_call(
         start_kernel,
@@ -324,11 +360,15 @@
     )(side, places, own_features, index)
 
     source = lax.all_to_all(weighted, GATHER, split_axis=0, concat_axis=0, tiled=True)
-    tile = pl.pallas_call(
+    kept = KEPT
+    tile, tile_near = pl.pallas_call(
         functools.partial(tile_kernel, sizes=sizes),
-        out_shape=jax.ShapeDtypeStruct((near, 2, own, far * own), bf16),
+        out_shape=(
+            jax.ShapeDtypeStruct((near - kept, 2, own, far * own), bf16),
+            jax.ShapeDtypeStruct((kept, 2, own, far * own), bf16),
+        ),
         in_specs=[VMEM, VMEM, pl.BlockSpec(memory_space=pl.ANY)],
-        out_specs=HBM,
+        out_specs=(HBM, VMEM),
         scratch_shapes=[
             pltpu.VMEM((FEATURES, far * own), bf16),
             pltpu.VMEM((own, far * own), f32),
@@ -344,18 +384,18 @@
     part = pl.pallas_call(
         functools.partial(second_kernel, node_count=count),
         out_shape=jax.ShapeDtypeStruct((far, 2, tx, own), bf16),
-        in_specs=[VMEM, HBM],
+        in_specs=[VMEM, HBM, VMEM],
         out_specs=VMEM,
         scratch_shapes=[
             pltpu.VMEM((2 * tx, near * own), bf16),
-            pltpu.VMEM((near, 2, own, far * own), bf16),
+            pltpu.VMEM((near - kept, 2, own, far * own), bf16),
             pltpu.VMEM((2 * tx, far * own), f32),
             pltpu.VMEM((2 * tx, far * own), f32),
-            pltpu.SemaphoreType.DMA((8,)),
+            pltpu.SemaphoreType.DMA(((near - kept) // 2,)),
         ],
         compiler_params=limit(50),
         name="second_wave",
-    )(source, tile)
+    )(source, tile, tile_near)
     parts = lax.all_to_all(part, REDUCE, split_axis=0, concat_axis=0, tiled=True)
     second, terms = pl.pallas_call(
         functools.partial(last_kernel, share=1.0 / (lanes * tx)),

time: 96.3 us -> 97.1 us (level)
  waiting for transfers between devices: 10 us -> 11.7 us
    all_to_all x1, waiting for transfers between devices: 1.21 us -> 2.9 us  [local(): lax.all_to_all(weighted, GATHER, split_axis=0, concat_axis=0, tiled=True)]
    pallas_call x1 -> x2, Pallas kernels: 12.7 us -> 12.4 us  [the longest x1 11 us: local(): pl.pallas_call(functools.partial(tile_kernel, sizes=sizes), out_shape=(ja...]
  transfers between devices with their start and end apart: 2 -> 2, of which waited for: 2 -> 2; matrix products, arithmetic and copies ran while one was open for 0% -> 0% of each run, Pallas kernels for 13% -> 11%
where the time goes in v4:
time: 97.1 us; the launch traced here: 96.7 us
  Pallas kernels  32.1 us (33%)
  blocking collectives  27.1 us (28%)
  starting transfers between devices  22 us (23%)
  waiting for transfers between devices  11.7 us (12%)
  local copies, waits for them, and re-layouts  2.01 us (2%)
  between operations  1.33 us (1%)
    all_to_all x1, blocking collectives, local(): lax.all_to_all(terms, 'freq', split_axis=0, concat_axis=0, tiled=True)  18.6 us
    all_to_all x1, starting transfers between devices, local(): lax.all_to_all(copies, BLK, split_axis=0, concat_axis=0, tiled=True)  17.8 us
    pallas_call x1, Pallas kernels, local(): pl.pallas_call(first_kernel, out_shape=(jax.ShapeDtypeStruct((2, tx, own)...  15 us
    pallas_call x1, Pallas kernels, local(): pl.pallas_call(functools.partial(tile_kernel, sizes=sizes), out_shape=(ja...  11 us
    all_to_all x1, waiting for transfers between devices, local(): lax.all_to_all(copies, BLK, split_axis=0, concat_axis=0, tiled=True)  8.77 us
    all_to_all x1, blocking collectives, local(): lax.all_to_all(part, REDUCE, split_axis=0, concat_axis=0, tiled=True)  8.5 us
    all_to_all x1, starting transfers between devices, local(): lax.all_to_all(weighted, GATHER, split_axis=0, concat_axis=0, tiled=True)  4.25 us
    pallas_call x1, Pallas kernels, local(): pl.pallas_call(functools.partial(second_kernel, node_count=count), out_sh...  3.97 us
  transfers between devices with their start and end apart: 2, of which 2 were waited for; matrix products, arithmetic and copies ran while one was open for 0% of the time, Pallas kernels for 11%

profile of v4, /device:TPU:1, one launch (start us, length us, event | category | flops | bytes accessed | tf_op | source)
XLA Modules:
  0.0 96.7 jit_solution(5354903363062521959)
XLA Ops:
  0.6 1.4 %copies.1 = bf16[128,3,128]{2,1,0:T(4,128)(2,1)} custom-call(s32[3,128]{1,0:T(4,128)} %node_ref.3), custom_call_target="tpu_custom_call" | custom-call | tf_op jit(solution)/shard_map/copies/pallas_call | solution.py:320
  2.0 17.8 %all-to-all-start = ((bf16[128,3,128]{2,1,0:T(4,128)(2,1)}), bf16[128,3,128]{2,1,0:T(4,128)(2,1)S(1)}, u32[]{:S(2)}, u32[]{:S(2)}) async-start(bf16[128,3,128]{2,1,0:T(4,128)(2,1)} %copies.1), calls=%async_computation | async-start | bytes 262144 | tf_op jit(solution)/shard_map/all_to_all | solution.py:328
  20.4 0.0 copy-start
  20.4 0.7 copy-done
  21.1 0.0 copy-start.1
  21.1 0.7 copy-done.1
  21.8 0.0 copy-start.2
  21.8 0.7 copy-done.2
  22.4 0.1 start.1
  22.5 8.8 %all-to-all-done.places_ref = bf16[128,3,128]{2,1,0:T(4,128)(2,1)S(1)} async-done(((bf16[128,3,128]{2,1,0:T(4,128)(2,1)}), bf16[128,3,128]{2,1,0:T(4,128)(2,1)S(1)}, u32[]{:S(2)}, u32[]{:S(2)}) %all-to-all-start) | async-done | bytes 98336 | tf_op jit(solution)/shard_map/all_to_all | solution.py:328
  31.3 15.0 %first_wave.1 = (f32[2,64,128]{2,1,0:T(8,128)S(1)}, bf16[16,2,64,128]{3,2,1,0:T(8,128)(2,1)}) custom-call(f32[8,128]{1,0:T(8,128)S(1)} %get-tuple-element.11.side_ref, bf16[128,3,128]{2,1,0:T(4,128)(2,1)S(1)} %all-to-all-done.places_ref, bf16[16,128]{1,0:T(8,128)(2,1)S(1)} %get-tuple-element.12.own_ref, s32[64,128]{1,0:T(8,128)S(1)} %get-tuple-element.13.index_ref), custom_call_target="tpu_custom_call" | custom-call | tf_op jit(solution)/shard_map/first_wave/pallas_call | solution.py:342
  46.3 4.2 %all-to-all-start.1 = ((bf16[16,2,64,128]{3,2,1,0:T(8,128)(2,1)}), bf16[16,2,64,128]{3,2,1,0:T(8,128)(2,1)}, u32[]{:S(2)}, u32[]{:S(2)}) async-start(bf16[16,2,64,128]{3,2,1,0:T(8,128)(2,1)} %get-tuple-element.14), calls=%async_computation.1 | async-start | bytes 1048576 | tf_op jit(solution)/shard_map/all_to_all | solution.py:362
  50.5 11.0 %green_tile.1 = (bf16[10,2,128,1024]{3,2,1,0:T(8,128)(2,1)}, bf16[6,2,128,1024]{3,2,1,0:T(8,128)(2,1)S(1)}) custom-call(f32[8,128]{1,0:T(8,128)S(1)} %get-tuple-element.11.side_ref, bf16[128,3,128]{2,1,0:T(4,128)(2,1)S(1)} %all-to-all-done.places_ref, f32[2,64,128]{2,1,0:T(8,128)S(1)} %get-tuple-element.15.after_ref.first_ref), custom_call_target="tpu_custom_call" | custom-call | flops 10000000000 | bytes 8388608 | tf_op jit(solution)/shard_map/green_tile/pallas_call | solution.py:364
  61.5 2.9 %all-to-all-done.1.source_ref = bf16[16,2,64,128]{3,2,1,0:T(8,128)(2,1)} async-done(((bf16[16,2,64,128]{3,2,1,0:T(8,128)(2,1)}), bf16[16,2,64,128]{3,2,1,0:T(8,128)(2,1)}, u32[]{:S(2)}, u32[]{:S(2)}) %all-to-all-start.1) | async-done | bytes 524320 | tf_op jit(solution)/shard_map/all_to_all | solution.py:362
  64.4 4.0 %second_wave.1 = bf16[8,2,64,128]{3,2,1,0:T(8,128)(2,1)S(1)} custom-call(bf16[16,2,64,128]{3,2,1,0:T(8,128)(2,1)} %all-to-all-done.1.source_ref, bf16[10,2,128,1024]{3,2,1,0:T(8,128)(2,1)} %get-tuple-element.16.tile_ref, bf16[6,2,128,1024]{3,2,1,0:T(8,128)(2,1)S(1)} %get-tuple-element.17.near_ref), custom_call_target="tpu_custom_call" | custom-call | tf_op jit(solution)/shard_map/second_wave/pallas_call | solution.py:384
  68.4 8.5 %all_to_all.20.parts_ref = bf16[8,2,64,128]{3,2,1,0:T(8,128)(2,1)S(1)} all-to-all(bf16[8,2,64,128]{3,2,1,0:T(8,128)(2,1)S(1)} %second_wave.1), channel_id=1, replica_groups=mesh['zs'=2,'za'=2,'y'=8,'x'=4,'freq'=4] {'za','x'}, dimensions={0} | all-to-all | bytes 524288 | tf_op jit(solution)/shard_map/all_to_all | solution.py:399
  76.9 0.7 last_sum.1
  77.6 18.6 %all_to_all.21 = f32[4,1,128]{2,1,0:T(1,128)S(1)} all-to-all(f32[4,1,128]{2,1,0:T(1,128)S(1)} %get-tuple-element.19), channel_id=1, replica_groups=mesh['zs'=2,'za'=2,'y'=8,'x'=4,'freq'=4] {'freq'}, dimensions={0} | all-to-all | bytes 4096 | tf_op jit(solution)/shard_map/all_to_all | solution.py:411
  96.2 0.5 reduce_sum.9
Async XLA Ops:
  2.0 29.3 %all-to-all-start = ((bf16[128,3,128]{2,1,0:T(4,128)(2,1)}), bf16[128,3,128]{2,1,0:T(4,128)(2,1)S(1)}, u32[]{:S(2)}, u32[]{:S(2)}) async-start(bf16[128,3,128]{2,1,0:T(4,128)(2,1)} %copies.1), calls=%async_computation | async-start | bytes 262144 | tf_op jit(solution)/shard_map/all_to_all | solution.py:328
  20.4 0.7 copy-start
  21.1 0.7 copy-start.1
  21.8 0.7 copy-start.2
  46.3 18.2 %all-to-all-start.1 = ((bf16[16,2,64,128]{3,2,1,0:T(8,128)(2,1)}), bf16[16,2,64,128]{3,2,1,0:T(8,128)(2,1)}, u32[]{:S(2)}, u32[]{:S(2)}) async-start(bf16[16,2,64,128]{3,2,1,0:T(8,128)(2,1)} %get-tuple-element.14), calls=%async_computation.1 | async-start | bytes 1048576 | tf_op jit(solution)/shard_map/all_to_all | solution.py:362

commit v5 on v4

--- a/solution.py
+++ b/solution.py
@@ -17,7 +17,7 @@
 FEATURES = 16
 SOFT = 0.0025 * GRID * GRID
 MAGIC = 12582912.0
-KEPT = 6
+KEPT = 4
 ROOT2 = math.sqrt(2.0)
 SIN_POLY = [ROOT2 * c for c in (3.1415820221197075, -5.167142794757069, 2.541899010399708, -0.554636148527055)]
 COS_POLY = [ROOT2 * c for c in (0.9999933001981278, -4.933938170377516, 4.04128504935244, -1.2221298133692595)]
@@ -74,11 +74,6 @@
 
 def dot(a, b, contract=((1,), (0,))):
     return lax.dot_general(a, b, (contract, ((), ())), preferred_element_type=jnp.float32)
-
-
-def copies_kernel(node_ref, copies_ref):
-    places = node_ref[...].astype(jnp.float32).astype(jnp.bfloat16)
-    copies_ref[...] = jnp.broadcast_to(places[None], copies_ref.shape)
 
 
 def start_kernel(wavenumber_ref, node_ref, emitters_ref, admittance_ref, own_ref, index_ref, side_ref):
@@ -271,13 +266,13 @@
         bring(p).start()
     for c in range(groups):
         lhs_ref[:, c * own : (c + 1) * own] = source_ref[c].reshape(2 * emitters, own)
-    for begin in [*range(far, groups, per), *range(0, far, per)]:
+    for begin, count in [(far, groups - far), *((p, per) for p in range(0, far, per))]:
         if begin < far:
             bring(begin // per).wait()
-        lhs = lhs_ref[:, begin * own : (begin + per) * own]
+        lhs = lhs_ref[:, begin * own : (begin + count) * own]
         for part, acc in ((0, acc_r), (1, acc_i)):
-            held = all_ref[begin : begin + per] if begin < far else near_ref[begin - far : begin - far + per]
-            here = dot(lhs, held[:, part].reshape(per * own, targets * own))
+            held = near_ref[:, part] if begin == far else all_ref[begin : begin + count, part]
+            here = dot(lhs, held.reshape(count * own, targets * own))
             acc[...] = here if begin == far else acc[...] + here
     scale = GRID * float(node_count) ** (-0.5)
     for b in range(targets):
@@ -317,14 +312,7 @@
     near, far = lax.axis_size(GATHER), lax.axis_size(REDUCE)
 
     f32, bf16 = jnp.float32, jnp.bfloat16
-    copies = pl.pallas_call(
-        copies_kernel,
-        out_shape=jax.ShapeDtypeStruct((blocks, *node_index.shape), bf16),
-        in_specs=[VMEM],
-        out_specs=VMEM,
-        compiler_params=limit(60),
-        name="copies",
-    )(node_index)
+    copies = jnp.broadcast_to(node_index.astype(bf16), (blocks, *node_index.shape))
     places = lax.all_to_all(copies, BLK, split_axis=0, concat_axis=0, tiled=True)
     own_features, index, side = pl.pallas_call(
         start_kernel,
@@ -391,7 +379,7 @@
             pltpu.VMEM((near - kept, 2, own, far * own), bf16),
             pltpu.VMEM((2 * tx, far * own), f32),
             pltpu.VMEM((2 * tx, far * own), f32),
-            pltpu.SemaphoreType.DMA(((near - kept) // 2,)),
+            pltpu.SemaphoreType.DMA((3,)),
         ],
         compiler_params=limit(50),
         name="second_wave",

time: 97.1 us -> 95.8 us (0.987)
  Pallas kernels: 32.1 us -> 30.4 us
    pallas_call x1 -> x0, Pallas kernels: 1.38 us -> none  [local(): pl.pallas_call(copies_kernel, out_shape=jax.ShapeDtypeStruct((blocks, *no...]
  transfers between devices with their start and end apart: 2 -> 2, of which waited for: 2 -> 2; matrix products, arithmetic and copies ran while one was open for 0% -> 0% of each run, Pallas kernels for 11% -> 12%
where the time goes in v5:
time: 95.8 us; the launch traced here: 95.4 us
  Pallas kernels  30.4 us (32%)
  blocking collectives  27.1 us (28%)
  starting transfers between devices  21.3 us (22%)
  waiting for transfers between devices  11.3 us (12%)
  local copies, waits for them, and re-layouts  2.7 us (3%)
  between operations  1.33 us (1%)
  other arithmetic  1.22 us (1%)
    all_to_all x1, blocking collectives, local(): lax.all_to_all(terms, 'freq', split_axis=0, concat_axis=0, tiled=True)  18.6 us
    all_to_all x1, starting transfers between devices, local(): lax.all_to_all(copies, BLK, split_axis=0, concat_axis=0, tiled=True)  17.8 us
    pallas_call x1, Pallas kernels, local(): pl.pallas_call(first_kernel, out_shape=(jax.ShapeDtypeStruct((2, tx, own)...  15 us
    pallas_call x1, Pallas kernels, local(): pl.pallas_call(functools.partial(tile_kernel, sizes=sizes), out_shape=(ja...  11.3 us
    all_to_all x1, waiting for transfers between devices, local(): lax.all_to_all(copies, BLK, split_axis=0, concat_axis=0, tiled=True)  8.77 us
    all_to_all x1, blocking collectives, local(): lax.all_to_all(part, REDUCE, split_axis=0, concat_axis=0, tiled=True)  8.5 us
    all_to_all x1, starting transfers between devices, local(): lax.all_to_all(weighted, GATHER, split_axis=0, concat_axis=0, tiled=True)  3.57 us
    pallas_call x1, Pallas kernels, local(): pl.pallas_call(functools.partial(second_kernel, node_count=count), out_sh...  3.37 us
  transfers between devices with their start and end apart: 2, of which 2 were waited for; matrix products, arithmetic and copies ran while one was open for 0% of the time, Pallas kernels for 12%

profile of v5, /device:TPU:1, one launch (start us, length us, event | category | flops | bytes accessed | tf_op | source)
XLA Modules:
  0.0 95.4 jit_solution(13958859627628983264)
XLA Ops:
  0.6 0.7 convert_element_type.3
  1.3 0.7 broadcast_in_dim.7
  2.0 17.8 %all-to-all-start = ((bf16[128,3,128]{2,1,0:T(4,128)(2,1)}), bf16[128,3,128]{2,1,0:T(4,128)(2,1)S(1)}, u32[]{:S(2)}, u32[]{:S(2)}) async-start(bf16[128,3,128]{2,1,0:T(4,128)(2,1)} %broadcast_in_dim.7), calls=%async_computation | async-start | bytes 262144 | tf_op jit(solution)/shard_map/all_to_all | solution.py:316
  20.4 0.0 copy-start
  20.4 0.7 copy-done
  21.1 0.0 copy-start.1
  21.1 0.7 copy-done.1
  21.8 0.0 copy-start.2
  21.8 0.7 copy-done.2
  22.4 0.1 start.1
  22.5 8.8 %all-to-all-done.places_ref = bf16[128,3,128]{2,1,0:T(4,128)(2,1)S(1)} async-done(((bf16[128,3,128]{2,1,0:T(4,128)(2,1)}), bf16[128,3,128]{2,1,0:T(4,128)(2,1)S(1)}, u32[]{:S(2)}, u32[]{:S(2)}) %all-to-all-start) | async-done | bytes 98336 | tf_op jit(solution)/shard_map/all_to_all | solution.py:316
  31.3 15.0 %first_wave.1 = (f32[2,64,128]{2,1,0:T(8,128)S(1)}, bf16[16,2,64,128]{3,2,1,0:T(8,128)(2,1)}) custom-call(f32[8,128]{1,0:T(8,128)S(1)} %get-tuple-element.11.side_ref, bf16[128,3,128]{2,1,0:T(4,128)(2,1)S(1)} %all-to-all-done.places_ref, bf16[16,128]{1,0:T(8,128)(2,1)S(1)} %get-tuple-element.12.own_ref, s32[64,128]{1,0:T(8,128)S(1)} %get-tuple-element.13.index_ref), custom_call_target="tpu_custom_call" | custom-call | tf_op jit(solution)/shard_map/first_wave/pallas_call | solution.py:330
  46.3 3.6 %all-to-all-start.1 = ((bf16[16,2,64,128]{3,2,1,0:T(8,128)(2,1)}), bf16[16,2,64,128]{3,2,1,0:T(8,128)(2,1)S(1)}, u32[]{:S(2)}, u32[]{:S(2)}) async-start(bf16[16,2,64,128]{3,2,1,0:T(8,128)(2,1)} %get-tuple-element.14), calls=%async_computation.1 | async-start | bytes 1048576 | tf_op jit(solution)/shard_map/all_to_all | solution.py:350
  49.9 11.3 %green_tile.1 = (bf16[12,2,128,1024]{3,2,1,0:T(8,128)(2,1)}, bf16[4,2,128,1024]{3,2,1,0:T(8,128)(2,1)S(1)}) custom-call(f32[8,128]{1,0:T(8,128)S(1)} %get-tuple-element.11.side_ref, bf16[128,3,128]{2,1,0:T(4,128)(2,1)S(1)} %all-to-all-done.places_ref, f32[2,64,128]{2,1,0:T(8,128)S(1)} %get-tuple-element.15.after_ref.first_ref), custom_call_target="tpu_custom_call" | custom-call | flops 10000000000 | bytes 8388608 | tf_op jit(solution)/shard_map/green_tile/pallas_call | solution.py:352
  61.2 2.5 %all-to-all-done.1.source_ref = bf16[16,2,64,128]{3,2,1,0:T(8,128)(2,1)S(1)} async-done(((bf16[16,2,64,128]{3,2,1,0:T(8,128)(2,1)}), bf16[16,2,64,128]{3,2,1,0:T(8,128)(2,1)S(1)}, u32[]{:S(2)}, u32[]{:S(2)}) %all-to-all-start.1) | async-done | bytes 524320 | tf_op jit(solution)/shard_map/all_to_all | solution.py:350
  63.7 3.4 %second_wave.1 = bf16[8,2,64,128]{3,2,1,0:T(8,128)(2,1)S(1)} custom-call(bf16[16,2,64,128]{3,2,1,0:T(8,128)(2,1)S(1)} %all-to-all-done.1.source_ref, bf16[12,2,128,1024]{3,2,1,0:T(8,128)(2,1)} %get-tuple-element.16.tile_ref, bf16[4,2,128,1024]{3,2,1,0:T(8,128)(2,1)S(1)} %get-tuple-element.17.near_ref), custom_call_target="tpu_custom_call" | custom-call | tf_op jit(solution)/shard_map/second_wave/pallas_call | solution.py:372
  67.1 8.5 %all_to_all.20.parts_ref = bf16[8,2,64,128]{3,2,1,0:T(8,128)(2,1)S(1)} all-to-all(bf16[8,2,64,128]{3,2,1,0:T(8,128)(2,1)S(1)} %second_wave.1), channel_id=1, replica_groups=mesh['zs'=2,'za'=2,'y'=8,'x'=4,'freq'=4] {'za','x'}, dimensions={0} | all-to-all | bytes 524288 | tf_op jit(solution)/shard_map/all_to_all | solution.py:387
  75.6 0.7 last_sum.1
  76.2 18.6 %all_to_all.21 = f32[4,1,128]{2,1,0:T(1,128)S(1)} all-to-all(f32[4,1,128]{2,1,0:T(1,128)S(1)} %get-tuple-element.19), channel_id=1, replica_groups=mesh['zs'=2,'za'=2,'y'=8,'x'=4,'freq'=4] {'freq'}, dimensions={0} | all-to-all | bytes 4096 | tf_op jit(solution)/shard_map/all_to_all | solution.py:399
  94.8 0.5 reduce_sum.9
Async XLA Ops:
  2.0 29.3 %all-to-all-start = ((bf16[128,3,128]{2,1,0:T(4,128)(2,1)}), bf16[128,3,128]{2,1,0:T(4,128)(2,1)S(1)}, u32[]{:S(2)}, u32[]{:S(2)}) async-start(bf16[128,3,128]{2,1,0:T(4,128)(2,1)} %broadcast_in_dim.7), calls=%async_computation | async-start | bytes 262144 | tf_op jit(solution)/shard_map/all_to_all | solution.py:316
  20.4 0.7 copy-start
  21.1 0.7 copy-start.1
  21.8 0.7 copy-start.2
  46.3 17.4 %all-to-all-start.1 = ((bf16[16,2,64,128]{3,2,1,0:T(8,128)(2,1)}), bf16[16,2,64,128]{3,2,1,0:T(8,128)(2,1)S(1)}, u32[]{:S(2)}, u32[]{:S(2)}) async-start(bf16[16,2,64,128]{3,2,1,0:T(8,128)(2,1)} %get-tuple-element.14), calls=%async_computation.1 | async-start | bytes 1048576 | tf_op jit(solution)/shard_map/all_to_all | solution.py:350

commit v6 on v5

--- a/solution.py
+++ b/solution.py
@@ -16,6 +16,18 @@
 LANES = 128
 FEATURES = 16
 SOFT = 0.0025 * GRID * GRID
+
+
+def bf16_parts(x, count):
+    parts = []
+    for _ in range(count):
+        mantissa, exponent = math.frexp(x)
+        parts.append(math.ldexp(round(mantissa * 256), exponent - 8))
+        x -= parts[-1]
+    return parts
+
+
+SOFT_PARTS = bf16_parts(SOFT, 3)
 MAGIC = 12582912.0
 KEPT = 4
 ROOT2 = math.sqrt(2.0)
@@ -30,11 +42,10 @@
     return total
 
 
-def green_parts(square, turns_per_step):
-    v = square + SOFT
+def green_parts(v, turns_per_step):
     inv = lax.rsqrt(v)
     turns = (v * inv) * turns_per_step
-    f = turns - ((turns + MAGIC) - MAGIC)
+    f = turns - lax.round(turns, lax.RoundingMethod.TO_NEAREST_EVEN)
     s = f * f
     half_sin = poly(SIN_POLY, s) * f
     half_cos = poly(COS_POLY, s)
@@ -52,10 +63,11 @@
     p = places.astype(jnp.float32) - 32.0
     high, low = split_norm(p)
     one = jnp.ones_like(high)
-    zero = jnp.zeros((FEATURES - 7, p.shape[1]), jnp.float32)
+    zero = jnp.zeros((FEATURES - 7 - len(SOFT_PARTS), p.shape[1]), jnp.float32)
     if target:
-        return jnp.concatenate([p, high, low, one, one, zero], axis=0)
-    return jnp.concatenate([p * -2.0, one, one, high, low, zero], axis=0)
+        return jnp.concatenate([p, high, low, *[one] * (2 + len(SOFT_PARTS)), zero], axis=0)
+    soft = [jnp.full_like(one, c) for c in SOFT_PARTS]
+    return jnp.concatenate([p * -2.0, one, one, high, low, *soft, zero], axis=0)
 
 
 def spread_features(x, y, z):
@@ -69,7 +81,7 @@
     out = jnp.where(lane == 2, z, out)
     out = jnp.where(lane == 3, high, out)
     out = jnp.where(lane == 4, low, out)
-    return jnp.where((lane == 5) | (lane == 6), 1.0, out)
+    return jnp.where((lane >= 5) & (lane < 7 + len(SOFT_PARTS)), 1.0, out)
 
 
 def dot(a, b, contract=((1,), (0,))):
@@ -86,11 +98,11 @@
 
 
 def first_kernel(side_ref, places_ref, own_ref, index_ref, first_ref, weighted_ref,
-                 rows_ref, d0, d1, g0, g1, acc_ref):
+                 rows_ref, c0, c1, g0, g1, acc_ref):
     blocks = places_ref.shape[0]
     own = own_ref.shape[1]
     emitters = index_ref.shape[0]
-    width = d0.shape[1]
+    width = c0.shape[1]
     per = width // own
     chunks = blocks // per
     turns = side_ref[6:7, 0:1]
@@ -109,32 +121,33 @@
 
     acc_ref[...] = jnp.zeros_like(acc_ref)
 
-    def distances(chunk, d_ref):
+    def columns(chunk, c_ref):
         for b in range(per):
-            psi = features(places_ref[chunk * per + b], False).astype(jnp.bfloat16)
-            d_ref[:, b * own : (b + 1) * own] = dot(rows_ref[:, 0:FEATURES], psi)
-
-    def tile(d_ref, g_ref):
-        for r in range(0, own + emitters, 16):
-            at = r if r < own else r + own
-            step = own if r < own else emitters
-            for w in range(0, width, 512):
-                real, imag = green_parts(d_ref[r : r + 16, w : w + 512], turns)
-                g_ref[at : at + 16, w : w + 512] = real.astype(jnp.bfloat16)
-                g_ref[at + step : at + step + 16, w : w + 512] = imag.astype(jnp.bfloat16)
+            psi = features(places_ref[chunk * per + b], False)
+            c_ref[:, b * own : (b + 1) * own] = psi.astype(jnp.bfloat16)
+
+    def tile(c_ref, g_ref):
+        for w in range(0, width, 256):
+            psi = c_ref[:, w : w + 256]
+            for r in range(0, own + emitters, 64):
+                at = r if r < own else r + own
+                step = own if r < own else emitters
+                real, imag = green_parts(dot(rows_ref[r : r + 64, 0:FEATURES], psi), turns)
+                g_ref[at : at + 64, w : w + 256] = real.astype(jnp.bfloat16)
+                g_ref[at + step : at + step + 64, w : w + 256] = imag.astype(jnp.bfloat16)
 
     def gather(g_ref):
         acc_ref[...] += dot(g_ref[2 * own :, :], g_ref[0 : 2 * own, :], ((1,), (1,)))
 
-    distances(0, d0)
+    columns(0, c0)
     g1[...] = jnp.zeros_like(g1)
 
     def pair(i, carry):
-        distances(2 * i + 1, d1)
-        tile(d0, g0)
+        columns(2 * i + 1, c1)
+        tile(c0, g0)
         gather(g1)
-        distances(jnp.minimum(2 * i + 2, chunks - 1), d0)
-        tile(d1, g1)
+        columns(jnp.minimum(2 * i + 2, chunks - 1), c0)
+        tile(c1, g1)
         gather(g0)
         return carry
 
@@ -337,8 +350,8 @@
         out_specs=(VMEM, VMEM),
         scratch_shapes=[
             pltpu.VMEM((own + tx, LANES), bf16),
-            pltpu.VMEM((own + tx, width), f32),
-            pltpu.VMEM((own + tx, width), f32),
+            pltpu.VMEM((FEATURES, width), bf16),
+            pltpu.VMEM((FEATURES, width), bf16),
             pltpu.VMEM((2 * (own + tx), width), bf16),
             pltpu.VMEM((2 * (own + tx), width), bf16),
             pltpu.VMEM((2 * tx, 2 * own), f32),

time: 95.8 us -> 94 us (0.981)
  Pallas kernels: 30.4 us -> 28.2 us
    pallas_call x1, Pallas kernels: 15 us -> 13.2 us  [local(): pl.pallas_call(first_kernel, out_shape=(jax.ShapeDtypeStruct((2, tx, own)...]
where the time goes in v6:
time: 94 us; the launch traced here: 93.6 us
  Pallas kernels  28.2 us (30%)
  blocking collectives  27.1 us (29%)
  starting transfers between devices  21.3 us (23%)
  waiting for transfers between devices  11.7 us (12%)
  local copies, waits for them, and re-layouts  2.7 us (3%)
  between operations  1.33 us (1%)
  other arithmetic  1.22 us (1%)
    all_to_all x1, blocking collectives, local(): lax.all_to_all(terms, 'freq', split_axis=0, concat_axis=0, tiled=True)  18.6 us
    all_to_all x1, starting transfers between devices, local(): lax.all_to_all(copies, BLK, split_axis=0, concat_axis=0, tiled=True)  17.8 us
    pallas_call x1, Pallas kernels, local(): pl.pallas_call(first_kernel, out_shape=(jax.ShapeDtypeStruct((2, tx, own)...  13.2 us
    pallas_call x1, Pallas kernels, local(): pl.pallas_call(functools.partial(tile_kernel, sizes=sizes), out_shape=(ja...  10.9 us
    all_to_all x1, waiting for transfers between devices, local(): lax.all_to_all(copies, BLK, split_axis=0, concat_axis=0, tiled=True)  8.77 us
    all_to_all x1, blocking collectives, local(): lax.all_to_all(part, REDUCE, split_axis=0, concat_axis=0, tiled=True)  8.5 us
    all_to_all x1, starting transfers between devices, local(): lax.all_to_all(weighted, GATHER, split_axis=0, concat_axis=0, tiled=True)  3.57 us
    pallas_call x1, Pallas kernels, local(): pl.pallas_call(functools.partial(second_kernel, node_count=count), out_sh...  3.37 us
  transfers between devices with their start and end apart: 2, of which 2 were waited for; matrix products, arithmetic and copies ran while one was open for 0% of the time, Pallas kernels for 12%

profile of v6, /device:TPU:1, one launch (start us, length us, event | category | flops | bytes accessed | tf_op | source)
XLA Modules:
  0.0 93.6 jit_solution(16539241174552147883)
XLA Ops:
  0.6 0.7 convert_element_type.3
  1.3 0.7 broadcast_in_dim.7
  2.0 17.8 %all-to-all-start = ((bf16[128,3,128]{2,1,0:T(4,128)(2,1)}), bf16[128,3,128]{2,1,0:T(4,128)(2,1)S(1)}, u32[]{:S(2)}, u32[]{:S(2)}) async-start(bf16[128,3,128]{2,1,0:T(4,128)(2,1)} %broadcast_in_dim.7), calls=%async_computation | async-start | bytes 262144 | tf_op jit(solution)/shard_map/all_to_all | solution.py:329
  20.4 0.0 copy-start
  20.4 0.7 copy-done
  21.1 0.0 copy-start.1
  21.1 0.7 copy-done.1
  21.8 0.0 copy-start.2
  21.8 0.7 copy-done.2
  22.4 0.1 start.1
  22.5 8.8 %all-to-all-done.places_ref = bf16[128,3,128]{2,1,0:T(4,128)(2,1)S(1)} async-done(((bf16[128,3,128]{2,1,0:T(4,128)(2,1)}), bf16[128,3,128]{2,1,0:T(4,128)(2,1)S(1)}, u32[]{:S(2)}, u32[]{:S(2)}) %all-to-all-start) | async-done | bytes 98336 | tf_op jit(solution)/shard_map/all_to_all | solution.py:329
  31.3 13.2 %first_wave.1 = (f32[2,64,128]{2,1,0:T(8,128)S(1)}, bf16[16,2,64,128]{3,2,1,0:T(8,128)(2,1)}) custom-call(f32[8,128]{1,0:T(8,128)S(1)} %get-tuple-element.11.side_ref, bf16[128,3,128]{2,1,0:T(4,128)(2,1)S(1)} %all-to-all-done.places_ref, bf16[16,128]{1,0:T(8,128)(2,1)S(1)} %get-tuple-element.12.own_ref, s32[64,128]{1,0:T(8,128)S(1)} %get-tuple-element.13.index_ref), custom_call_target="tpu_custom_call" | custom-call | tf_op jit(solution)/shard_map/first_wave/pallas_call | solution.py:343
  44.5 3.6 %all-to-all-start.1 = ((bf16[16,2,64,128]{3,2,1,0:T(8,128)(2,1)}), bf16[16,2,64,128]{3,2,1,0:T(8,128)(2,1)S(1)}, u32[]{:S(2)}, u32[]{:S(2)}) async-start(bf16[16,2,64,128]{3,2,1,0:T(8,128)(2,1)} %get-tuple-element.14), calls=%async_computation.1 | async-start | bytes 1048576 | tf_op jit(solution)/shard_map/all_to_all | solution.py:363
  48.1 10.9 %green_tile.1 = (bf16[12,2,128,1024]{3,2,1,0:T(8,128)(2,1)}, bf16[4,2,128,1024]{3,2,1,0:T(8,128)(2,1)S(1)}) custom-call(f32[8,128]{1,0:T(8,128)S(1)} %get-tuple-element.11.side_ref, bf16[128,3,128]{2,1,0:T(4,128)(2,1)S(1)} %all-to-all-done.places_ref, f32[2,64,128]{2,1,0:T(8,128)S(1)} %get-tuple-element.15.after_ref.first_ref), custom_call_target="tpu_custom_call" | custom-call | flops 10000000000 | bytes 8388608 | tf_op jit(solution)/shard_map/green_tile/pallas_call | solution.py:365
  59.0 2.9 %all-to-all-done.1.source_ref = bf16[16,2,64,128]{3,2,1,0:T(8,128)(2,1)S(1)} async-done(((bf16[16,2,64,128]{3,2,1,0:T(8,128)(2,1)}), bf16[16,2,64,128]{3,2,1,0:T(8,128)(2,1)S(1)}, u32[]{:S(2)}, u32[]{:S(2)}) %all-to-all-start.1) | async-done | bytes 524320 | tf_op jit(solution)/shard_map/all_to_all | solution.py:363
  61.9 3.4 %second_wave.1 = bf16[8,2,64,128]{3,2,1,0:T(8,128)(2,1)S(1)} custom-call(bf16[16,2,64,128]{3,2,1,0:T(8,128)(2,1)S(1)} %all-to-all-done.1.source_ref, bf16[12,2,128,1024]{3,2,1,0:T(8,128)(2,1)} %get-tuple-element.16.tile_ref, bf16[4,2,128,1024]{3,2,1,0:T(8,128)(2,1)S(1)} %get-tuple-element.17.near_ref), custom_call_target="tpu_custom_call" | custom-call | tf_op jit(solution)/shard_map/second_wave/pallas_call | solution.py:385
  65.3 8.5 %all_to_all.20.parts_ref = bf16[8,2,64,128]{3,2,1,0:T(8,128)(2,1)S(1)} all-to-all(bf16[8,2,64,128]{3,2,1,0:T(8,128)(2,1)S(1)} %second_wave.1), channel_id=1, replica_groups=mesh['zs'=2,'za'=2,'y'=8,'x'=4,'freq'=4] {'za','x'}, dimensions={0} | all-to-all | bytes 524288 | tf_op jit(solution)/shard_map/all_to_all | solution.py:400
  73.8 0.7 last_sum.1
  74.5 18.6 %all_to_all.21 = f32[4,1,128]{2,1,0:T(1,128)S(1)} all-to-all(f32[4,1,128]{2,1,0:T(1,128)S(1)} %get-tuple-element.19), channel_id=1, replica_groups=mesh['zs'=2,'za'=2,'y'=8,'x'=4,'freq'=4] {'freq'}, dimensions={0} | all-to-all | bytes 4096 | tf_op jit(solution)/shard_map/all_to_all | solution.py:412
  93.1 0.5 reduce_sum.9
Async XLA Ops:
  2.0 29.3 %all-to-all-start = ((bf16[128,3,128]{2,1,0:T(4,128)(2,1)}), bf16[128,3,128]{2,1,0:T(4,128)(2,1)S(1)}, u32[]{:S(2)}, u32[]{:S(2)}) async-start(bf16[128,3,128]{2,1,0:T(4,128)(2,1)} %broadcast_in_dim.7), calls=%async_computation | async-start | bytes 262144 | tf_op jit(solution)/shard_map/all_to_all | solution.py:329
  20.4 0.7 copy-start
  21.1 0.7 copy-start.1
  21.8 0.7 copy-start.2
  44.5 17.4 %all-to-all-start.1 = ((bf16[16,2,64,128]{3,2,1,0:T(8,128)(2,1)}), bf16[16,2,64,128]{3,2,1,0:T(8,128)(2,1)S(1)}, u32[]{:S(2)}, u32[]{:S(2)}) async-start(bf16[16,2,64,128]{3,2,1,0:T(8,128)(2,1)} %get-tuple-element.14), calls=%async_computation.1 | async-start | bytes 1048576 | tf_op jit(solution)/shard_map/all_to_all | solution.py:363

commit v7 on v6

--- a/solution.py
+++ b/solution.py
@@ -10,9 +10,9 @@
 from jax.sharding import PartitionSpec as P
 
 GRID = 64
-BLK = ("zs", "za", "y", "x")
-GATHER = ("zs", "y")
-REDUCE = ("za", "x")
+BLK = ("zs", "za", "ys", "ya", "x")
+GATHER = ("za", "ya", "x")
+REDUCE = ("zs", "ys")
 LANES = 128
 FEATURES = 16
 SOFT = 0.0025 * GRID * GRID
@@ -195,25 +195,25 @@
 
     def distances(c, d_ref):
         block = block_at({**here, **unravel(c, GATHER, sizes)}, sizes)
-        psi = jnp.transpose(features(places_ref[block], False)).astype(jnp.bfloat16)
-        d_ref[...] = dot(psi, cols_ref[...])
+        d_ref[:, 0:FEATURES] = jnp.transpose(features(places_ref[block], False)).astype(jnp.bfloat16)
 
     def tile(d_ref, store):
-        for r in range(0, own, 16):
-            for w in range(0, width, 512):
-                real, imag = green_parts(d_ref[r : r + 16, w : w + 512], turns)
+        for w in range(0, width, 256):
+            targets = cols_ref[:, w : w + 256]
+            for r in range(0, own, 64):
+                real, imag = green_parts(dot(d_ref[r : r + 64, 0:FEATURES], targets), turns)
                 store(0, r, w, real.astype(jnp.bfloat16))
                 store(1, r, w, imag.astype(jnp.bfloat16))
 
     def into(t_ref):
         def store(p, r, w, value):
-            t_ref[p, r : r + 16, w : w + 512] = value
+            t_ref[p, r : r + 64, w : w + 256] = value
 
         return store
 
     def kept(c):
         def store(p, r, w, value):
-            near_ref[c, p, r : r + 16, w : w + 512] = value
+            near_ref[c, p, r : r + 64, w : w + 256] = value
 
         return store
 
@@ -372,8 +372,8 @@
         out_specs=(HBM, VMEM),
         scratch_shapes=[
             pltpu.VMEM((FEATURES, far * own), bf16),
-            pltpu.VMEM((own, far * own), f32),
-            pltpu.VMEM((own, far * own), f32),
+            pltpu.VMEM((own, LANES), bf16),
+            pltpu.VMEM((own, LANES), bf16),
             pltpu.VMEM((2, own, far * own), bf16),
             pltpu.VMEM((2, own, far * own), bf16),
             pltpu.SemaphoreType.DMA((2, 2, 2)),
@@ -392,7 +392,7 @@
             pltpu.VMEM((near - kept, 2, own, far * own), bf16),
             pltpu.VMEM((2 * tx, far * own), f32),
             pltpu.VMEM((2 * tx, far * own), f32),
-            pltpu.SemaphoreType.DMA((3,)),
+            pltpu.SemaphoreType.DMA((6,)),
         ],
         compiler_params=limit(50),
         name="second_wave",
@@ -414,7 +414,7 @@
 
 
 def solution(mesh):
-    split = Mesh(mesh.devices.reshape(2, 2, 8, 4, mesh.shape["freq"]), (*BLK, "freq"))
+    split = Mesh(mesh.devices.reshape(2, 2, 4, 2, 4, mesh.shape["freq"]), (*BLK, "freq"))
     in_specs = (P(None, BLK), P(), P(None, BLK), P("freq"))
     out_specs = (P("freq", None, None, BLK), P(BLK))
     return jax.shard_map(local, mesh=split, in_specs=in_specs, out_specs=out_specs, check_vma=False)

time: 94 us -> 93.1 us (level)
  blocking collectives: 27.1 us -> 30.1 us
  waiting for transfers between devices: 11.7 us -> 8.77 us
  Pallas kernels: 28.2 us -> 27.2 us
    all_to_all x1, blocking collectives: 8.5 us -> 11.8 us  [local(): lax.all_to_all(part, REDUCE, split_axis=0, concat_axis=0, tiled=True)]
    all_to_all x1, waiting for transfers between devices: 2.91 us -> 0.01 us  [local(): lax.all_to_all(weighted, GATHER, split_axis=0, concat_axis=0, tiled=True)]
  transfers between devices with their start and end apart: 2 -> 2, of which waited for: 2 -> 1; matrix products, arithmetic and copies ran while one was open for 0% -> 0% of each run, Pallas kernels for 12% -> 11%
where the time goes in v7:
time: 93.1 us; the launch traced here: 92.6 us
  blocking collectives  30.1 us (32%)
  Pallas kernels  27.2 us (29%)
  starting transfers between devices  21.3 us (23%)
  waiting for transfers between devices  8.77 us (9%)
  local copies, waits for them, and re-layouts  2.7 us (3%)
  between operations  1.34 us (1%)
  other arithmetic  1.22 us (1%)
    all_to_all x1, blocking collectives, local(): lax.all_to_all(terms, 'freq', split_axis=0, concat_axis=0, tiled=True)  18.3 us
    all_to_all x1, starting transfers between devices, local(): lax.all_to_all(copies, BLK, split_axis=0, concat_axis=0, tiled=True)  17.8 us
    pallas_call x1, Pallas kernels, local(): pl.pallas_call(first_kernel, out_shape=(jax.ShapeDtypeStruct((2, tx, own)...  13.2 us
    all_to_all x1, blocking collectives, local(): lax.all_to_all(part, REDUCE, split_axis=0, concat_axis=0, tiled=True)  11.8 us
    pallas_call x1, Pallas kernels, local(): pl.pallas_call(functools.partial(tile_kernel, sizes=sizes), out_shape=(ja...  10 us
    all_to_all x1, waiting for transfers between devices, local(): lax.all_to_all(copies, BLK, split_axis=0, concat_axis=0, tiled=True)  8.77 us
    all_to_all x1, starting transfers between devices, local(): lax.all_to_all(weighted, GATHER, split_axis=0, concat_axis=0, tiled=True)  3.57 us
    pallas_call x1, Pallas kernels, local(): pl.pallas_call(functools.partial(second_kernel, node_count=count), out_sh...  3.21 us
  transfers between devices with their start and end apart: 2, of which 1 were waited for; matrix products, arithmetic and copies ran while one was open for 0% of the time, Pallas kernels for 11%

profile of v7, /device:TPU:1, one launch (start us, length us, event | category | flops | bytes accessed | tf_op | source)
XLA Modules:
  0.0 92.6 jit_solution(3327370114910750327)
XLA Ops:
  0.6 0.7 convert_element_type.3
  1.3 0.7 broadcast_in_dim.7
  2.0 17.8 %all-to-all-start = ((bf16[128,3,128]{2,1,0:T(4,128)(2,1)}), bf16[128,3,128]{2,1,0:T(4,128)(2,1)S(1)}, u32[]{:S(2)}, u32[]{:S(2)}) async-start(bf16[128,3,128]{2,1,0:T(4,128)(2,1)} %broadcast_in_dim.7), calls=%async_computation | async-start | bytes 262144 | tf_op jit(solution)/shard_map/all_to_all | solution.py:329
  20.4 0.0 copy-start
  20.4 0.7 copy-done
  21.1 0.0 copy-start.1
  21.1 0.7 copy-done.1
  21.8 0.0 copy-start.2
  21.8 0.7 copy-done.2
  22.4 0.1 start.1
  22.5 8.8 %all-to-all-done.places_ref = bf16[128,3,128]{2,1,0:T(4,128)(2,1)S(1)} async-done(((bf16[128,3,128]{2,1,0:T(4,128)(2,1)}), bf16[128,3,128]{2,1,0:T(4,128)(2,1)S(1)}, u32[]{:S(2)}, u32[]{:S(2)}) %all-to-all-start) | async-done | bytes 98336 | tf_op jit(solution)/shard_map/all_to_all | solution.py:329
  31.3 13.2 %first_wave.1 = (f32[2,64,128]{2,1,0:T(8,128)S(1)}, bf16[16,2,64,128]{3,2,1,0:T(8,128)(2,1)}) custom-call(f32[8,128]{1,0:T(8,128)S(1)} %get-tuple-element.11.side_ref, bf16[128,3,128]{2,1,0:T(4,128)(2,1)S(1)} %all-to-all-done.places_ref, bf16[16,128]{1,0:T(8,128)(2,1)S(1)} %get-tuple-element.12.own_ref, s32[64,128]{1,0:T(8,128)S(1)} %get-tuple-element.13.index_ref), custom_call_target="tpu_custom_call" | custom-call | tf_op jit(solution)/shard_map/first_wave/pallas_call | solution.py:343
  44.5 3.6 %all-to-all-start.1 = ((bf16[16,2,64,128]{3,2,1,0:T(8,128)(2,1)}), bf16[16,2,64,128]{3,2,1,0:T(8,128)(2,1)S(1)}, u32[]{:S(2)}, u32[]{:S(2)}) async-start(bf16[16,2,64,128]{3,2,1,0:T(8,128)(2,1)} %get-tuple-element.14), calls=%async_computation.1 | async-start | bytes 1048576 | tf_op jit(solution)/shard_map/all_to_all | solution.py:363
  48.1 10.0 %green_tile.1 = (bf16[12,2,128,1024]{3,2,1,0:T(8,128)(2,1)}, bf16[4,2,128,1024]{3,2,1,0:T(8,128)(2,1)S(1)}) custom-call(f32[8,128]{1,0:T(8,128)S(1)} %get-tuple-element.11.side_ref, bf16[128,3,128]{2,1,0:T(4,128)(2,1)S(1)} %all-to-all-done.places_ref, f32[2,64,128]{2,1,0:T(8,128)S(1)} %get-tuple-element.15.after_ref.first_ref), custom_call_target="tpu_custom_call" | custom-call | flops 10000000000 | bytes 8388608 | tf_op jit(solution)/shard_map/green_tile/pallas_call | solution.py:365
  58.1 0.0 all-to-all-done.1.source_ref
  58.1 3.2 %second_wave.1 = bf16[8,2,64,128]{3,2,1,0:T(8,128)(2,1)S(1)} custom-call(bf16[16,2,64,128]{3,2,1,0:T(8,128)(2,1)S(1)} %all-to-all-done.1.source_ref, bf16[12,2,128,1024]{3,2,1,0:T(8,128)(2,1)} %get-tuple-element.16.tile_ref, bf16[4,2,128,1024]{3,2,1,0:T(8,128)(2,1)S(1)} %get-tuple-element.17.near_ref), custom_call_target="tpu_custom_call" | custom-call | tf_op jit(solution)/shard_map/second_wave/pallas_call | solution.py:385
  61.4 11.8 %all_to_all.20.parts_ref = bf16[8,2,64,128]{3,2,1,0:T(8,128)(2,1)S(1)} all-to-all(bf16[8,2,64,128]{3,2,1,0:T(8,128)(2,1)S(1)} %second_wave.1), channel_id=1, replica_groups=mesh['zs'=2,'za'=2,'ys'=4,'ya'=2,'x'=4,'freq'=4] {'zs','ys'}, dimensions={0} | all-to-all | bytes 524288 | tf_op jit(solution)/shard_map/all_to_all | solution.py:400
  73.2 0.7 last_sum.1
  73.8 18.3 %all_to_all.21 = f32[4,1,128]{2,1,0:T(1,128)S(1)} all-to-all(f32[4,1,128]{2,1,0:T(1,128)S(1)} %get-tuple-element.19), channel_id=1, replica_groups=mesh['zs'=2,'za'=2,'ys'=4,'ya'=2,'x'=4,'freq'=4] {'freq'}, dimensions={0} | all-to-all | bytes 4096 | tf_op jit(solution)/shard_map/all_to_all | solution.py:412
  92.1 0.5 reduce_sum.9
Async XLA Ops:
  2.0 29.3 %all-to-all-start = ((bf16[128,3,128]{2,1,0:T(4,128)(2,1)}), bf16[128,3,128]{2,1,0:T(4,128)(2,1)S(1)}, u32[]{:S(2)}, u32[]{:S(2)}) async-start(bf16[128,3,128]{2,1,0:T(4,128)(2,1)} %broadcast_in_dim.7), calls=%async_computation | async-start | bytes 262144 | tf_op jit(solution)/shard_map/all_to_all | solution.py:329
  20.4 0.7 copy-start
  21.1 0.7 copy-start.1
  21.8 0.7 copy-start.2
  44.5 13.6 %all-to-all-start.1 = ((bf16[16,2,64,128]{3,2,1,0:T(8,128)(2,1)}), bf16[16,2,64,128]{3,2,1,0:T(8,128)(2,1)S(1)}, u32[]{:S(2)}, u32[]{:S(2)}) async-start(bf16[16,2,64,128]{3,2,1,0:T(8,128)(2,1)} %get-tuple-element.14), calls=%async_computation.1 | async-start | bytes 1048576 | tf_op jit(solution)/shard_map/all_to_all | solution.py:363
